TPU v7x, 8 devices: a whole 2x2x1 slice. The times are simulated.
8 devices in a mesh: dp: 1 (over z), tp: 8 (over y, x, core).
Axes of the slice: x: 2, y: 2, z: 1, core: 2. Of those that a mesh axis runs over, the one named last changes fastest.
Arguments:
- x: bfloat16 [256, 2048], P('dp')
- cache_len: int32 [256], P('dp')
- k_cache: bfloat16 [2, 256, 32, 128, 64], P(None, 'dp', 'tp')
- v_cache: bfloat16 [2, 256, 32, 128, 64], P(None, 'dp', 'tp')
- norm_gain: float32 [2, 2, 2048], replicated
- norm_bias: float32 [2, 2, 2048], replicated
- w_qkv: bfloat16 [2, 2048, 3, 32, 64], P(None, None, None, 'tp')
- b_qkv: bfloat16 [2, 3, 32, 64], P(None, None, 'tp')
- w_out: bfloat16 [2, 32, 64, 2048], P(None, 'tp')
- b_out: bfloat16 [2, 2048], replicated
- w_up: bfloat16 [2, 2048, 8192], P(None, None, 'tp')
- b_up: bfloat16 [2, 8192], P(None, 'tp')
- w_down: bfloat16 [2, 8192, 2048], P(None, 'tp')
- b_down: bfloat16 [2, 2048], replicated
Outputs:
- output 1: bfloat16 [256, 2048], P('dp')
- output 2: bfloat16 [2, 256, 32, 128, 64], P(None, 'dp', 'tp')
- output 3: bfloat16 [2, 256, 32, 128, 64], P(None, 'dp', 'tp')
All inputs are finite; a program needn't handle non-finite values.
Results may differ from a plain program's by a relative error of at most 0.0166233.
Values are sent between devices in bfloat16 or wider.
A program may use at most 1 GiB of HBM per device.

v0:
```python
import jax
import jax.numpy as jnp
from jax import lax
from jax.sharding import PartitionSpec as P

NORM_EPS = 1e-5


def layer_norm(vec, gain_vec, bias_vec):
    vec_f = vec.astype(jnp.float32)
    row_mean = jnp.mean(vec_f, axis=-1, keepdims=True)
    centered = vec_f - row_mean
    row_var = jnp.mean(centered * centered, axis=-1, keepdims=True)
    return (centered * lax.rsqrt(row_var + NORM_EPS) * gain_vec + bias_vec).astype(jnp.bfloat16)


def solution(mesh):
    cache_spec = P(None, 'dp', 'tp', None, None)
    in_specs = (P('dp', None), P('dp'), cache_spec, cache_spec, P(), P(),
                P(None, None, None, 'tp', None), P(None, None, 'tp', None),
                P(None, 'tp', None, None), P(), P(None, None, 'tp'), P(None, 'tp'),
                P(None, 'tp', None), P())
    out_specs = (P('dp', None), cache_spec, cache_spec)

    def local_step(x, cache_len, k_cache, v_cache, norm_gain, norm_bias, w_qkv, b_qkv, w_out, b_out, w_up, b_up, w_down, b_down):
        num_layers = k_cache.shape[0]
        smax = k_cache.shape[3]
        head_dim = k_cache.shape[4]
        slots = jnp.arange(smax)
        write_here = slots[None, None, :, None] == cache_len[:, None, None, None]
        visible = slots[None, None, :] <= cache_len[:, None, None]
        scale = head_dim ** -0.5
        k_layers = []
        v_layers = []
        for layer in range(num_layers):
            hidden = layer_norm(x, norm_gain[layer, 0], norm_bias[layer, 0])
            qkv_all = (jnp.einsum('bc,cthd->bthd', hidden, w_qkv[layer], preferred_element_type=jnp.float32) + b_qkv[layer].astype(jnp.float32)).astype(jnp.bfloat16)
            k_layer = jnp.where(write_here, qkv_all[:, 1, :, None, :], k_cache[layer])
            v_layer = jnp.where(write_here, qkv_all[:, 2, :, None, :], v_cache[layer])
            scores = jnp.einsum('bhd,bhjd->bhj', qkv_all[:, 0], k_layer, preferred_element_type=jnp.float32) * scale
            scores = jnp.where(visible, scores, -1e30)
            attn_prob = jax.nn.softmax(scores, axis=-1).astype(jnp.bfloat16)
            attended = jnp.einsum('bhj,bhjd->bhd', attn_prob, v_layer, preferred_element_type=jnp.float32).astype(jnp.bfloat16)
            attn_part = jnp.einsum('bhd,hdc->bc', attended, w_out[layer], preferred_element_type=jnp.float32).astype(jnp.bfloat16)
            attn_sum = lax.psum(attn_part, 'tp')
            x_mid = (x.astype(jnp.float32) + attn_sum.astype(jnp.float32) + b_out[layer].astype(jnp.float32)).astype(jnp.bfloat16)
            hidden_mlp = layer_norm(x_mid, norm_gain[layer, 1], norm_bias[layer, 1])
            up_act = jnp.maximum(jnp.dot(hidden_mlp, w_up[layer], preferred_element_type=jnp.float32) + b_up[layer].astype(jnp.float32), 0.0).astype(jnp.bfloat16)
            mlp_part = jnp.dot(up_act, w_down[layer], preferred_element_type=jnp.float32).astype(jnp.bfloat16)
            mlp_sum = lax.psum(mlp_part, 'tp')
            x = (x_mid.astype(jnp.float32) + mlp_sum.astype(jnp.float32) + b_down[layer].astype(jnp.float32)).astype(jnp.bfloat16)
            k_layers.append(k_layer)
            v_layers.append(v_layer)
        return x, jnp.stack(k_layers), jnp.stack(v_layers)

    return jax.shard_map(local_step, mesh=mesh, in_specs=in_specs, out_specs=out_specs, check_vma=False)
```

profile of v0, /device:TPU:0, one launch (start us, length us, event | category | flops | bytes accessed | tf_op | source)
XLA Modules:
  0.0 291.5 jit_solution(8927756610324151802)
XLA Ops:
  7.2 0.0 all-reduce.5.cloned.1.call-start
  7.2 1.4 convert_reduce_fusion.3
  8.7 1.6 fusion.60
  10.3 0.7 bitcast_convert_fusion.4
  11.0 0.8 fusion.176
  11.9 0.8 fusion.177
  12.7 0.8 iota_compare_fusion.1
  13.5 0.0 copy-start
  13.5 5.4 %fusion.175 = (bf16[1,2048,3,4,64]{1,4,3,2,0:T(8,128)(2,1)S(1)}, bf16[1,2048,3,4,64]{1,4,3,2,0:T(8,128)(2,1)}) fusion(bf16[2,2048,3,4,64]{1,4,3,2,0:T(8,128)(2,1)} %param.20), kind=kLoop, calls=%fused_computation.188 | loop fusion | bytes 12582912 | tf_op jit(solution)/shard_map/slice | solution.py:37
  18.9 0.0 copy-done
  18.9 1.1 fusion.100
  20.1 0.2 add_convert_fusion.1
  20.3 0.2 copy.25
  20.5 0.2 copy.26
  20.7 0.0 copy-start.2
  20.7 0.4 copy.33
  21.1 12.9 %fusion.7 = f32[256,4,1,128]{3,2,1,0:T(1,128)S(1)} fusion(bf16[256,4,64,1]{2,3,1,0:T(2,128)(2,1)S(1)} %copy.33, pred[256,128]{1,0:T(8,128)(4,1)S(1)} %get-tuple-element.40, bf16[2,256,4,128,64]{3,4,2,1,0:T(8,128)(2,1)} %param.16, bf16[256,4,64]{2,1,0:T(4,128)(2,1)S(1)} %copy.25), kind=kOutput, calls=%fused_computation.13 | convolution fusion | flops 25165824 | bytes 17596416 | tf_op jit(solution)/shard_map/bhd,bhjd->bhj/dot_general | solution.py:40
  34.0 0.4 fusion.98
  34.4 0.0 copy-done.2
  34.4 11.8 %fusion.6 = bf16[256,4,1,64]{3,2,1,0:T(2,128)(2,1)S(1)} fusion(pred[256,128]{1,0:T(8,128)(4,1)S(1)} %get-tuple-element.40, bf16[2,256,4,128,64]{3,4,2,1,0:T(8,128)(2,1)} %param.17, bf16[256,4,64]{2,1,0:T(4,128)(2,1)S(1)} %copy.26, bf16[256,4,128,1]{2,0,1,3:T(8,128)(2,1)S(1)} %fusion.98), kind=kOutput, calls=%fused_computation.11 | convolution fusion | flops 25165824 | bytes 17334272 | tf_op jit(solution)/shard_map/bhj,bhjd->bhd/dot_general | solution.py:43
  46.2 0.0 copy-start.6
  46.2 0.0 copy-start.4
  46.2 0.4 copy.36
  46.6 2.7 fusion.32
  49.3 0.0 all-reduce.5.cloned.1.call-update
  49.3 0.0 all-reduce.7.cloned.1.call-start
  49.4 0.0 copy-done.6
  49.4 0.0 copy-done.4
  49.4 48.1 %all-reduce.5.cloned.1.call-done = bf16[256,2048]{1,0:T(8,128)(2,1)} async-done(((bf16[256,2048]{1,0:T(8,128)(2,1)}), bf16[256,2048]{1,0:T(8,128)(2,1)}) %all-reduce.5.cloned.1.call-update) | async-done | bytes 1048592 | tf_op jit(solution)/shard_map/psum | solution.py:45
  97.5 1.7 convert_reduce_fusion.2
  99.2 0.4 fusion.56
  99.7 0.0 copy-start.5
  99.7 6.8 %fusion.34 = bf16[256,2048]{1,0:T(8,128)(2,1)} fusion(bf16[2,1024,2048]{2,1,0:T(8,128)(2,1)} %param.26, bf16[2,2048,1024]{2,1,0:T(8,128)(2,1)} %param.24, bf16[256,2048]{1,0:T(8,128)(2,1)S(1)} %get-tuple-element.8, f32[2048]{0:T(1024)S(1)} %bitcast.145, f32[2048]{0:T(1024)S(1)} %bitcast.144, f32[256]{0:T(256)S(1)} %add_rsqrt_fusion.2, ...), kind=kOutput, calls=%fused_computation.58 | convolution fusion | flops 2151940096 | bytes 10508288 | tf_op jit(solution)/shard_map/dot_general | solution.py:49
  106.5 0.0 all-reduce.7.cloned.1.call-update
  106.5 0.2 all-reduce.9.cloned.1.call-start
  106.8 0.0 copy-done.5
  106.8 44.4 %all-reduce.7.cloned.1.call-done = bf16[256,2048]{1,0:T(8,128)(2,1)} async-done(((bf16[256,2048]{1,0:T(8,128)(2,1)}), bf16[256,2048]{1,0:T(8,128)(2,1)}) %all-reduce.7.cloned.1.call-update) | async-done | bytes 1048592 | tf_op jit(solution)/shard_map/psum | solution.py:50
  151.2 0.0 copy-start.1
  151.2 1.9 convert_reduce_fusion.1
  153.1 0.4 fusion.52
  153.6 0.0 copy-done.1
  153.6 1.2 fusion.103
  154.7 0.2 add_convert_fusion
  155.0 0.2 copy.27
  155.1 0.2 copy.28
  155.3 0.4 copy.37
  155.8 12.9 %fusion.5 = f32[256,4,1,128]{3,2,1,0:T(1,128)S(1)} fusion(bf16[256,4,64,1]{2,3,1,0:T(2,128)(2,1)S(1)} %copy.37, pred[256,128]{1,0:T(8,128)(4,1)S(1)} %get-tuple-element.40, bf16[2,256,4,128,64]{3,4,2,1,0:T(8,128)(2,1)} %param.16, bf16[256,4,64]{2,1,0:T(4,128)(2,1)S(1)} %copy.27), kind=kOutput, calls=%fused_computation.9 | convolution fusion | flops 25165824 | bytes 17596416 | tf_op jit(solution)/shard_map/bhd,bhjd->bhj/dot_general | solution.py:40
  168.6 0.4 fusion.99
  169.0 11.8 %fusion.4 = bf16[256,4,1,64]{3,2,1,0:T(2,128)(2,1)S(1)} fusion(pred[256,128]{1,0:T(8,128)(4,1)S(1)} %get-tuple-element.40, bf16[2,256,4,128,64]{3,4,2,1,0:T(8,128)(2,1)} %param.17, bf16[256,4,64]{2,1,0:T(4,128)(2,1)S(1)} %copy.28, bf16[256,4,128,1]{2,0,1,3:T(8,128)(2,1)S(1)} %fusion.99), kind=kOutput, calls=%fused_computation.7 | convolution fusion | flops 25165824 | bytes 17334272 | tf_op jit(solution)/shard_map/bhj,bhjd->bhd/dot_general | solution.py:43
  180.8 0.0 copy-start.3
  180.8 0.4 copy.40
  181.3 2.7 fusion.33
  183.9 0.0 all-reduce.9.cloned.1.call-update
  184.0 0.0 all-reduce.11.cloned.1.call-start
  184.0 0.0 copy-done.3
  184.0 43.9 %broadcast_select_fusion.1 = (bf16[1,256,4,128,64]{3,4,2,1,0:T(8,128)(2,1)}, bf16[1,256,4,128,64]{3,4,2,1,0:T(8,128)(2,1)}, bf16[1,256,4,128,64]{3,4,2,1,0:T(8,128)(2,1)}, bf16[1,256,4,128,64]{3,4,2,1,0:T(8,128)(2,1)}) fusion(pred[256,128]{1,0:T(8,128)(4,1)S(1)} %get-tuple-element.40, bf16[2,256,4,128,64]{3,4,2,1,0:T(8,128)(2,1)} %param.17, ...), kind=kLoop, calls=%fused_computation.15 | loop fusion | flops 33554432 | bytes 134774784 | tf_op jit(solution)/shard_map/jit(_where)/select_n | solution.py:39
  227.9 0.7 all-reduce.9.cloned.1.call-done
  228.6 1.7 convert_reduce_fusion
  230.4 0.4 fusion.48
  230.8 6.8 %fusion.37 = bf16[256,2048]{1,0:T(8,128)(2,1)} fusion(bf16[2,1024,2048]{2,1,0:T(8,128)(2,1)} %param.26, bf16[2,2048,1024]{2,1,0:T(8,128)(2,1)} %param.24, bf16[256,2048]{1,0:T(8,128)(2,1)S(1)} %get-tuple-element.4, f32[2048]{0:T(1024)S(1)} %bitcast.141, f32[2048]{0:T(1024)S(1)} %bitcast.140, f32[256]{0:T(256)S(1)} %add_rsqrt_fusion, ...), kind=kOutput, calls=%fused_computation.59 | convolution fusion | flops 2151940096 | bytes 10508288 | tf_op jit(solution)/shard_map/dot_general | solution.py:49
  237.7 0.0 all-reduce.11.cloned.1.call-update
  237.7 43.7 %pad_maximum_fusion = (bf16[2,256,4,128,64]{3,4,2,1,0:T(8,128)(2,1)}, bf16[2,256,4,128,64]{3,4,2,1,0:T(8,128)(2,1)}) fusion(bf16[1,256,4,128,64]{3,4,2,1,0:T(8,128)(2,1)} %get-tuple-element.21, bf16[1,256,4,128,64]{3,4,2,1,0:T(8,128)(2,1)} %get-tuple-element.22, bf16[1,256,4,128,64]{3,4,2,1,0:T(8,128)(2,1)} %get-tuple-element.10, ...), kind=kLoop, calls=%fused_computation.4 | loop fusion | flops 33554432 | bytes 134217728 | tf_op jit(solution)/shard_map/stack | solution.py:54
  281.4 0.9 all-reduce.11.cloned.1.call-done
  282.4 2.6 fusion.71
  (13 shorter events, 0.2 us)
Async XLA Ops:
  7.2 90.3 %all-reduce.5.cloned.1.call-start = ((), (), s32[]{:S(2)}) async-start(), calls=%async_computation | async-start | bytes 2097152 | tf_op jit(solution)/shard_map/psum | solution.py:45
  13.5 5.5 %copy-start = (bf16[256,2048]{1,0:T(8,128)(2,1)S(1)}, bf16[256,2048]{1,0:T(8,128)(2,1)}, u32[]{:S(2)}) copy-start(bf16[256,2048]{1,0:T(8,128)(2,1)} %param.14) | copy-start | bytes 3145732
  20.7 13.7 %copy-start.2 = (bf16[256,4,64]{2,1,0:T(4,128)(2,1)}, bf16[256,4,64]{2,1,0:T(4,128)(2,1)S(1)}, u32[]{:S(2)}) copy-start(bf16[256,4,64]{2,1,0:T(4,128)(2,1)S(1)} %copy.26) | copy-start | bytes 393220
  46.2 3.2 %copy-start.6 = (bf16[2,1024]{1,0:T(2,128)(2,1)S(1)}, bf16[2,1024]{1,0:T(2,128)(2,1)}, u32[]{:S(2)}) copy-start(bf16[2,1024]{1,0:T(2,128)(2,1)} %param.25) | copy-start | bytes 12292
  46.2 3.2 %copy-start.4 = (bf16[2,2048]{1,0:T(2,128)(2,1)S(1)}, bf16[2,2048]{1,0:T(2,128)(2,1)}, u32[]{:S(2)}) copy-start(bf16[2,2048]{1,0:T(2,128)(2,1)} %param.23) | copy-start | bytes 24580
  49.3 101.9 %all-reduce.7.cloned.1.call-start = ((), (), s32[]{:S(2)}) async-start(), calls=%async_computation.1 | async-start | bytes 2097152 | tf_op jit(solution)/shard_map/psum | solution.py:50
  99.7 7.1 %copy-start.5 = (bf16[2,2048]{1,0:T(2,128)(2,1)S(1)}, bf16[2,2048]{1,0:T(2,128)(2,1)}, u32[]{:S(2)}) copy-start(bf16[2,2048]{1,0:T(2,128)(2,1)} %param.27) | copy-start | bytes 24580
  106.5 122.1 %all-reduce.9.cloned.1.call-start = ((), (), s32[]{:S(2)}) async-start(), calls=%async_computation.2 | async-start | bytes 2097152 | tf_op jit(solution)/shard_map/psum | solution.py:45
  151.2 2.3 copy-start.1
  180.8 3.2 %copy-start.3 = (bf16[256,4,64]{2,1,0:T(4,128)(2,1)S(1)}, bf16[256,4,64]{2,1,0:T(4,128)(2,1)}, u32[]{:S(2)}) copy-start(bf16[256,4,64]{2,1,0:T(4,128)(2,1)} %copy-done.2) | copy-start | bytes 393220
  184.0 98.4 %all-reduce.11.cloned.1.call-start = ((), (), s32[]{:S(2)}) async-start(), calls=%async_computation.3 | async-start | bytes 2097152 | tf_op jit(solution)/shard_map/psum | solution.py:50
Sparse Core Ops, SparseCore 0:
  49.4 48.0 all-reduce.4
  106.7 44.5 all-reduce.6
  184.1 44.5 all-reduce.8
  237.8 44.5 all-reduce.10
where the time goes:
time: 292 us; the launch traced here: 291 us
  other arithmetic  103 us (35%)
  waiting for transfers between devices  94.2 us (32%)
  matrix products  70.6 us (24%)
  between operations  14 us (5%)
  local copies, waits for them, and re-layouts  9.63 us (3%)
    psum x2, waiting for transfers between devices, local_step(): attn_sum = lax.psum(attn_part, 'tp')  48.8 us
    psum x2, waiting for transfers between devices, local_step(): mlp_sum = lax.psum(mlp_part, 'tp')  45.4 us
    select_n x1, other arithmetic, local_step(): v_layer = jnp.where(write_here, qkv_all[:, 2, :, None, :], v_cache[layer])  43.9 us
    another operation x1, other arithmetic, local_step(): return (x, jnp.stack(k_layers), jnp.stack(v_layers))  43.7 us
    dot_general x2, matrix products, local_step(): jnp.einsum('bhd,bhjd->bhj', qkv_all[:, 0], k_layer, preferred_element_typ...  25.7 us
    dot_general x2, matrix products, local_step(): jnp.einsum('bhj,bhjd->bhd', attn_prob, v_layer, preferred_element_type=jn...  23.6 us
    dot_general x2, matrix products, local_step(): jnp.dot(up_act, w_down[layer], preferred_element_type=jnp.float32)  13.7 us
    reduce_sum x4, other arithmetic, layer_norm(): row_mean = jnp.mean(vec_f, axis=-1, keepdims=True)  6.8 us
  transfers between devices with their start and end apart: 4, of which 4 were waited for; matrix products, arithmetic and copies ran while one was open for 30% of the time, Pallas kernels for 0%

commit v1 on v0

v1 whole, which is shorter than its diff:
```python
import functools

import jax
import jax.numpy as jnp
from jax import lax
from jax.experimental import pallas as pl
from jax.experimental.pallas import tpu as pltpu
from jax.sharding import PartitionSpec as P

NORM_EPS = 1e-5
MESH = pl.DeviceIdType.MESH
F32 = jnp.float32
BF16 = jnp.bfloat16
NT = (((1,), (1,)), ((), ()))
NN = (((1,), (0,)), ((), ()))

GROUP = 16
CHUNKS = 2


def dot(lhs, rhs, dims=NN):
    return lax.dot_general(lhs, rhs, dims, preferred_element_type=F32)


def norm(rows, gain, bias):
    mean = jnp.mean(rows, axis=-1, keepdims=True)
    centered = rows - mean
    var = jnp.mean(centered * centered, axis=-1, keepdims=True)
    return centered * lax.rsqrt(var + NORM_EPS) * gain + bias


def attention_kernel(layer, lens, x_ref, gain_ref, bias_ref, bqkv_ref, wqkv_hbm, wout_hbm, k_hbm, v_hbm, *rest):
    if layer > 0:
        rest = rest[2:]
    (ko_hbm, vo_hbm, part_ref, kbuf, vbuf, wqkv, wout, hbuf, ktb, vtb, qbuf, abuf,
     w_sem, k_sem, v_sem, ko_sem, vo_sem) = rest
    batch, width = x_ref.shape
    hd = wout.shape[0]
    head = hd // 4
    slots = kbuf.shape[2]
    groups = batch // GROUP

    w_copy = pltpu.make_async_copy(wqkv_hbm.at[layer], wqkv, w_sem.at[0])
    w_copy.start()

    def load(src, buf, sem, g):
        rows = pl.ds(g * GROUP, GROUP)
        return pltpu.make_async_copy(src.at[layer, rows], buf.at[rows], sem.at[g])

    def save(buf, dst, sem, g):
        rows = pl.ds(g * GROUP, GROUP)
        return pltpu.make_async_copy(buf.at[rows], dst.at[layer, rows], sem.at[g])

    def start_loads(g, carry):
        load(k_hbm, kbuf, k_sem, g).start()
        load(v_hbm, vbuf, v_sem, g).start()
        return carry

    lax.fori_loop(0, groups, start_loads, 0)
    o_copy = pltpu.make_async_copy(wout_hbm.at[layer], wout, w_sem.at[1])
    o_copy.start()

    if layer == 0:
        gain = gain_ref[0:1, :]
        bias = bias_ref[0:1, :]

        def norm_rows(i, carry):
            rows = pl.ds(i * 32, 32)
            hbuf[rows, :] = norm(x_ref[rows, :].astype(F32), gain, bias).astype(BF16)
            return carry

        lax.fori_loop(0, batch // 32, norm_rows, 0)
    else:
        hbuf[...] = x_ref[...]
    w_copy.wait()
    hidden = hbuf[...]
    qbuf[...] = (dot(hidden, wqkv[0:hd, :], NT) + bqkv_ref[layer:layer + 1, 0:hd].astype(F32)).astype(BF16)
    for part, pages in ((1, ktb), (2, vtb)):
        row = bqkv_ref[layer:layer + 1, part * hd:(part + 1) * hd].astype(F32)
        column = jnp.broadcast_to(row, (128, hd)).T
        for half in range(batch // 128):
            cols = dot(wqkv[part * hd:(part + 1) * hd, :], hbuf[half * 128:(half + 1) * 128, :], NT) + column
            for j in range(128 // GROUP):
                turned = cols if j == 0 else pltpu.roll(cols, 128 - j * GROUP, 1)
                pages[half * (128 // GROUP) + j] = turned.astype(BF16)

    n = GROUP * 4
    lane8 = lax.broadcasted_iota(jnp.int32, (8, slots), 1)
    top8 = lax.broadcasted_iota(jnp.int32, (8, slots), 0) < 4
    lane_hd = lax.broadcasted_iota(jnp.int32, (hd, slots), 1)
    own_head = (lax.broadcasted_iota(jnp.int32, (n, hd), 0) % 4) == (lax.broadcasted_iota(jnp.int32, (n, hd), 1) // head)
    repeat = ((lax.broadcasted_iota(jnp.int32, (n, GROUP), 0) // 4) == lax.broadcasted_iota(jnp.int32, (n, GROUP), 1)).astype(F32).astype(BF16)
    gather = ((lax.broadcasted_iota(jnp.int32, (GROUP, n), 1) // 4) == lax.broadcasted_iota(jnp.int32, (GROUP, n), 0)).astype(F32).astype(BF16)
    scale = head ** -0.5

    def step(g, carry):
        base = g * GROUP
        rows = pl.ds(pl.multiple_of(base, GROUP), GROUP)
        qrep = jnp.where(own_head, dot(repeat, qbuf[rows, :]), 0.0).astype(BF16)
        load(k_hbm, kbuf, k_sem, g).wait()
        kt = ktb[g].astype(F32)
        probs = []
        for i in range(0, GROUP, 2):
            tiles = []
            for b in (i, i + 1):
                column = jnp.broadcast_to(kt[:, b:b + 1], (hd, slots)).astype(BF16)
                tile = jnp.where(lane_hd == lens[base + b], column, kbuf[base + b])
                kbuf[base + b] = tile
                tiles.append(tile)
            both = dot(qrep[i * 4:i * 4 + 8, :], jnp.concatenate(tiles, axis=1))
            score = jnp.where(top8, both[:, 0:slots], both[:, slots:2 * slots]) * scale
            limit = jnp.where(top8, lens[base + i], lens[base + i + 1])
            probs.append(jnp.where(lane8 <= limit, score, -1e30))
        save(kbuf, ko_hbm, ko_sem, g).start()
        scores = jnp.concatenate(probs, axis=0)
        top = jnp.max(scores, axis=-1, keepdims=True)
        weights = jnp.exp(scores - top)
        prob = weights / jnp.sum(weights, axis=-1, keepdims=True)
        load(v_hbm, vbuf, v_sem, g).wait()
        vt = vtb[g].astype(F32)
        outs = []
        for i in range(0, GROUP, 2):
            tiles = []
            for b in (i, i + 1):
                column = jnp.broadcast_to(vt[:, b:b + 1], (hd, slots)).astype(BF16)
                tile = jnp.where(lane_hd == lens[base + b], column, vbuf[base + b])
                vbuf[base + b] = tile
                tiles.append(tile)
            pair = prob[i * 4:i * 4 + 8, :]
            spread = jnp.concatenate([jnp.where(top8, pair, 0.0), jnp.where(top8, 0.0, pair)], axis=1).astype(BF16)
            outs.append(dot(spread, jnp.concatenate(tiles, axis=1), NT))
        save(vbuf, vo_hbm, vo_sem, g).start()
        heads = jnp.where(own_head, jnp.concatenate(outs, axis=0), 0.0).astype(BF16)
        abuf[rows, :] = dot(gather, heads).astype(BF16)
        return carry

    lax.fori_loop(0, groups, step, 0)
    o_copy.wait()
    part_ref[...] = dot(abuf[...], wout[...]).astype(BF16)

    def finish(g, carry):
        save(kbuf, ko_hbm, ko_sem, g).wait()
        save(vbuf, vo_hbm, vo_sem, g).wait()
        return carry

    lax.fori_loop(0, groups, finish, 0)


def attention(layer, lens, x, gains, biases, bqkv, wqkv, wout, k_in, v_in, k_out=None, v_out=None):
    batch, width = x.shape
    hd = wout.shape[1]
    slots = k_in.shape[3]
    groups = batch // GROUP
    any_spec = pl.BlockSpec(memory_space=pl.ANY)
    vmem_spec = pl.BlockSpec(memory_space=pltpu.VMEM)
    args = [lens, x, gains, biases, bqkv, wqkv, wout, k_in, v_in]
    specs = [pl.BlockSpec(memory_space=pltpu.SMEM)] + [vmem_spec] * 4 + [any_spec] * 4
    alias = {}
    if layer > 0:
        args += [k_out, v_out]
        specs += [any_spec] * 2
        alias = {9: 0, 10: 1}
    return pl.pallas_call(
        functools.partial(attention_kernel, layer),
        out_shape=(
            jax.ShapeDtypeStruct(k_in.shape, BF16),
            jax.ShapeDtypeStruct(v_in.shape, BF16),
            jax.ShapeDtypeStruct((batch, width), BF16),
        ),
        in_specs=specs,
        out_specs=(any_spec, any_spec, vmem_spec),
        input_output_aliases=alias,
        scratch_shapes=[
            pltpu.VMEM((batch, hd, slots), BF16),
            pltpu.VMEM((batch, hd, slots), BF16),
            pltpu.VMEM((3 * hd, width), BF16),
            pltpu.VMEM((hd, width), BF16),
            pltpu.VMEM((batch, width), BF16),
            pltpu.VMEM((groups, hd, 128), BF16),
            pltpu.VMEM((groups, hd, 128), BF16),
            pltpu.VMEM((batch, hd), BF16),
            pltpu.VMEM((batch, hd), BF16),
            pltpu.SemaphoreType.DMA((2,)),
            pltpu.SemaphoreType.DMA((groups,)),
            pltpu.SemaphoreType.DMA((groups,)),
            pltpu.SemaphoreType.DMA((groups,)),
            pltpu.SemaphoreType.DMA((groups,)),
        ],
        compiler_params=pltpu.CompilerParams(vmem_limit_bytes=60 * 1024 * 1024),
        name=f"attention_{layer}",
    )(*args)


def mlp_kernel(layer, last, part_ref, x_ref, gain_ref, bias_ref, bout_ref, bup_ref, bdown_ref, wup_hbm, wdown_hbm,
               full_ref, own_ref, wup, wdown, part2, hbuf, ubuf, pair_in, cross_out, cross_in, own_sum, xown,
               w_sem, pair_s, pair_r, cross_s, cross_r, gat_s, gat_r, fwd_s, fwd_r):
    batch, width = part_ref.shape
    hidden = wup.shape[1]
    rows_c = batch // CHUNKS
    rows_o = rows_c // 8
    me = lax.axis_index("tp")
    core = lax.rem(me, 2)
    chip = lax.div(me, 2)
    cx = lax.rem(chip, 2)
    cy = lax.div(chip, 2)
    partner = chip * 2 + 1 - core
    chips = ((1 - cy) * 2 + 1 - cx, cy * 2 + 1 - cx, (1 - cy) * 2 + cx, chip)

    def device(index):
        return {"tp": index}

    def rows_of(c, owner):
        return pl.ds(pl.multiple_of(c * rows_c + owner * rows_o, rows_o), rows_o)

    copies = [
        pltpu.make_async_copy(wup_hbm.at[layer], wup, w_sem.at[0]),
        pltpu.make_async_copy(wdown_hbm.at[layer], wdown, w_sem.at[1]),
    ]
    for copy in copies:
        copy.start()
    if layer == 0:
        x_copies = [pltpu.make_async_copy(x_ref.at[rows_of(c, me)], xown.at[c], w_sem.at[2 + c]) for c in range(CHUNKS)]
        for copy in x_copies:
            copy.start()

    barrier = pltpu.get_barrier_semaphore()
    for peer in (partner,) + tuple(t * 2 + core for t in chips[:3]):
        pl.semaphore_signal(barrier, inc=1, device_id=device(peer), device_id_type=MESH)
    pl.semaphore_wait(barrier, 4)

    def remote(src, dst, send, recv, target):
        return pltpu.make_async_remote_copy(
            src_ref=src, dst_ref=dst, send_sem=send, recv_sem=recv, device_id=device(target), device_id_type=MESH)

    def pair_copy(s, c, k):
        src = part_ref if s == 0 else part2
        return remote(src.at[rows_of(c, chips[k] * 2 + 1 - core)], pair_in.at[s, c, k],
                      pair_s.at[s, c, k], pair_r.at[s, c, k], partner)

    def cross_copy(s, c, k):
        return remote(cross_out.at[s, c, k], cross_in.at[s, c, k],
                      cross_s.at[s, c, k], cross_r.at[s, c, k], chips[k] * 2 + core)

    def gather_copy(s, c, k):
        rows = rows_of(c, me)
        target = partner if k == 3 else chips[k] * 2 + core
        return remote(hbuf.at[s, rows], hbuf.at[s, rows], gat_s.at[s, c, k], gat_r.at[s, c, k], target)

    def forward_copy(s, c, k):
        rows = rows_of(c, chips[k] * 2 + core)
        return remote(hbuf.at[s, rows], hbuf.at[s, rows], fwd_s.at[s, c, k], fwd_r.at[s, c, k], partner)

    def send_pairs(s, c):
        for k in range(4):
            pair_copy(s, c, k).start()

    def add_pairs(s, c):
        src = part_ref if s == 0 else part2
        for k in range(4):
            pair_copy(s, c, k).wait_recv()
            both = src[rows_of(c, chips[k] * 2 + core), :].astype(F32) + pair_in[s, c, k].astype(F32)
            if k < 3:
                cross_out[s, c, k] = both.astype(BF16)
                cross_copy(s, c, k).start()
            else:
                own_sum[c] = both

    def own_total(s, c):
        total = own_sum[c]
        for k in (1, 2, 0):
            cross_copy(s, c, k).wait_recv()
            total = total + cross_in[s, c, k].astype(F32)
        return total

    def send_own(s, c):
        for k in range(4):
            gather_copy(s, c, k).start()

    def forward(s, c):
        for k in (1, 2, 0):
            gather_copy(s, c, k).wait_recv()
            forward_copy(s, c, k).start()

    def arrived(s, c):
        gather_copy(s, c, 3).wait_recv()
        for k in range(3):
            forward_copy(s, c, k).wait_recv()

    def row(ref, index):
        return ref[index:index + 1, :].astype(F32)

    def first_finish(c):
        total = own_total(0, c)
        old = xown[c] if layer == 0 else x_ref[c]
        mid = (old.astype(F32) + total + row(bout_ref, layer)).astype(BF16)
        xown[c] = mid
        hbuf[0, rows_of(c, me), :] = norm(mid.astype(F32), row(gain_ref, 2 * layer + 1), row(bias_ref, 2 * layer + 1)).astype(BF16)
        send_own(0, c)

    def second_finish(c):
        total = own_total(1, c)
        new = (xown[c].astype(F32) + total + row(bdown_ref, layer)).astype(BF16)
        if last:
            hbuf[1, rows_of(c, me), :] = new
        else:
            own_ref[c] = new
            hbuf[1, rows_of(c, me), :] = norm(new.astype(F32), row(gain_ref, 2 * layer + 2), row(bias_ref, 2 * layer + 2)).astype(BF16)
        send_own(1, c)

    def mlp(c):
        rows = slice(c * rows_c, (c + 1) * rows_c)
        h = hbuf[0, rows, :]
        for n in range(0, hidden, 256):
            up = dot(h, wup[:, n:n + 256]) + bup_ref[layer:layer + 1, n:n + 256].astype(F32)
            ubuf[:, n:n + 256] = jnp.maximum(up, 0.0).astype(BF16)
        u = ubuf[...]
        for n in range(0, width, 256):
            part2[rows, n:n + 256] = dot(u, wdown[:, n:n + 256]).astype(BF16)

    for c in range(CHUNKS):
        send_pairs(0, c)
    for c in range(CHUNKS):
        add_pairs(0, c)
    if layer == 0:
        for copy in x_copies:
            copy.wait()
    for c in range(CHUNKS):
        first_finish(c)
    for copy in copies:
        copy.wait()
    for c in range(CHUNKS):
        forward(0, c)
        if c > 0:
            add_pairs(1, c - 1)
        arrived(0, c)
        mlp(c)
        send_pairs(1, c)
    add_pairs(1, CHUNKS - 1)
    for c in range(CHUNKS):
        second_finish(c)
    for c in range(CHUNKS):
        forward(1, c)
    for c in range(CHUNKS):
        arrived(1, c)
        rows = slice(c * rows_c, (c + 1) * rows_c)
        full_ref[rows, :] = hbuf[1, rows, :]
    if last:
        own_ref[...] = jnp.zeros_like(own_ref)
    for s in range(2):
        for c in range(CHUNKS):
            for k in range(4):
                pair_copy(s, c, k).wait_send()
                gather_copy(s, c, k).wait_send()
                if k < 3:
                    cross_copy(s, c, k).wait_send()
                    forward_copy(s, c, k).wait_send()


def mlp_block(layer, last, part, x, gains, biases, bout, bup, bdown, wup, wdown):
    batch, width = part.shape
    hidden = wup.shape[2]
    rows_o = batch // CHUNKS // 8
    any_spec = pl.BlockSpec(memory_space=pl.ANY)
    vmem_spec = pl.BlockSpec(memory_space=pltpu.VMEM)
    own = (CHUNKS, rows_o, width)
    own_shape = own if not last else (8, 128)
    dma = pltpu.SemaphoreType.DMA
    return pl.pallas_call(
        functools.partial(mlp_kernel, layer, last),
        out_shape=(jax.ShapeDtypeStruct((batch, width), BF16), jax.ShapeDtypeStruct(own_shape, BF16)),
        in_specs=[vmem_spec, any_spec if layer == 0 else vmem_spec] + [vmem_spec] * 5 + [any_spec] * 2,
        out_specs=(vmem_spec, vmem_spec),
        scratch_shapes=[
            pltpu.VMEM((width, hidden), BF16),
            pltpu.VMEM((hidden, width), BF16),
            pltpu.VMEM((batch, width), BF16),
            pltpu.VMEM((2, batch, width), BF16),
            pltpu.VMEM((batch // CHUNKS, hidden), BF16),
            pltpu.VMEM((2, CHUNKS, 4, rows_o, width), BF16),
            pltpu.VMEM((2, CHUNKS, 3, rows_o, width), BF16),
            pltpu.VMEM((2, CHUNKS, 3, rows_o, width), BF16),
            pltpu.VMEM(own, F32),
            pltpu.VMEM(own, BF16),
            dma((2 + CHUNKS,)),
            dma((2, CHUNKS, 4)),
            dma((2, CHUNKS, 4)),
            dma((2, CHUNKS, 3)),
            dma((2, CHUNKS, 3)),
            dma((2, CHUNKS, 4)),
            dma((2, CHUNKS, 4)),
            dma((2, CHUNKS, 3)),
            dma((2, CHUNKS, 3)),
        ],
        compiler_params=pltpu.CompilerParams(
            collective_id=layer, has_side_effects=True, vmem_limit_bytes=60 * 1024 * 1024),
        name=f"mlp_{layer}",
    )(part, x, gains, biases, bout, bup, bdown, wup, wdown)


def solution(mesh):
    cache_spec = P(None, 'dp', 'tp', None, None)
    in_specs = (P('dp', None), P('dp'), cache_spec, cache_spec, P(), P(),
                P(None, None, None, 'tp', None), P(None, None, 'tp', None),
                P(None, 'tp', None, None), P(), P(None, None, 'tp'), P(None, 'tp'),
                P(None, 'tp', None), P())
    out_specs = (P('dp', None), cache_spec, cache_spec)

    def local_step(x, cache_len, k_cache, v_cache, norm_gain, norm_bias, w_qkv, b_qkv, w_out, b_out, w_up, b_up, w_down, b_down):
        layers, batch, heads, slots, head = k_cache.shape
        width = x.shape[1]
        hd = heads * head
        k_in = jnp.swapaxes(k_cache, 3, 4).reshape(layers, batch, hd, slots)
        v_in = jnp.swapaxes(v_cache, 3, 4).reshape(layers, batch, hd, slots)
        wqkv = jnp.transpose(w_qkv, (0, 2, 3, 4, 1)).reshape(layers, 3 * hd, width)
        bqkv = b_qkv.reshape(layers, 3 * hd)
        wout = w_out.reshape(layers, hd, width)
        gains = norm_gain.reshape(2 * layers, width)
        biases = norm_bias.reshape(2 * layers, width)

        k_out = v_out = None
        rows, own = x, x
        for layer in range(layers):
            extra = () if layer == 0 else (k_out, v_out)
            k_out, v_out, part = attention(layer, cache_len, rows, gains, biases, bqkv, wqkv, wout, k_in, v_in, *extra)
            rows, own = mlp_block(layer, layer == layers - 1, part, own, gains, biases, b_out, b_up, b_down, w_up, w_down)

        def back(cache):
            return jnp.swapaxes(cache.reshape(layers, batch, heads, head, slots), 3, 4)

        return rows, back(k_out), back(v_out)

    return jax.shard_map(local_step, mesh=mesh, in_specs=in_specs, out_specs=out_specs, check_vma=False)
```

time: 292 us -> 141 us (0.48)
  Pallas kernels: 0 us -> 134 us
  other arithmetic: 103 us -> 0 us
  waiting for transfers between devices: 94.2 us -> 0 us
  matrix products: 70.6 us -> 0 us
  between operations: 14 us -> 0.66 us
  local copies, waits for them, and re-layouts: 9.63 us -> 6.45 us
    pallas_call x0 -> x4, Pallas kernels: none -> 134 us  [the longest x2 72.5 us: mlp_block(): pl.pallas_call(functools.partial(mlp_kernel, layer, last), out_shape=(jax...]
    psum x4 -> x0, waiting for transfers between devices: 94.2 us -> none  [the longest x2 48.8 us: local_step(): attn_sum = lax.psum(attn_part, 'tp')]
    dot_general x8 -> x0, matrix products: 68.3 us -> none  [the longest x2 25.7 us: local_step(): jnp.einsum('bhd,bhjd->bhj', qkv_all[:, 0], k_layer, preferred_element_typ...]
    select_n x1 -> x0, other arithmetic: 43.9 us -> none  [local_step(): v_layer = jnp.where(write_here, qkv_all[:, 2, :, None, :], v_cache[layer])]
    another operation x1 -> x0, other arithmetic: 43.7 us -> none  [local_step(): return (x, jnp.stack(k_layers), jnp.stack(v_layers))]
    reduce_sum x8 -> x0, other arithmetic: 9.71 us -> none  [the longest x4 6.8 us: layer_norm(): row_mean = jnp.mean(vec_f, axis=-1, keepdims=True)]
    slice x3 -> x0, local copies, waits for them, and re-layouts: 7.1 us -> none  [the longest x1 5.45 us: local_step(): w_qkv[layer]]
    reshape x0 -> x3, local copies, waits for them, and re-layouts: none -> 4.15 us  [the longest x1 1.4 us: local_step(): biases = norm_bias.reshape(2 * layers, width)]
  transfers between devices with their start and end apart: 4 -> 0, of which waited for: 4 -> 0; matrix products, arithmetic and copies ran while one was open for 30% -> 0% of each run, Pallas kernels for 0% -> 0%
where the time goes in v1:
time: 141 us
  Pallas kernels  134 us (95%)
  local copies, waits for them, and re-layouts  6.45 us (5%)
    pallas_call x2, Pallas kernels, mlp_block(): pl.pallas_call(functools.partial(mlp_kernel, layer, last), out_shape=(jax...  72.5 us
    pallas_call x2, Pallas kernels, attention(): pl.pallas_call(functools.partial(attention_kernel, layer), out_shape=(jax...  61.1 us

profile of v1, /device:TPU:0, one launch (start us, length us, event | category | flops | bytes accessed | tf_op | source)
XLA Modules:
  0.0 140.7 jit_solution(4763847455911569194)
XLA Ops:
  0.6 1.4 reshape.35.bqkv_ref
  2.0 1.4 reshape.33.gain_ref
  3.4 1.4 reshape.34.bias_ref
  4.8 30.6 %attention_0.1 = (bf16[2,256,256,128]{3,2,1,0:T(8,128)(2,1)}, bf16[2,256,256,128]{3,2,1,0:T(8,128)(2,1)}, bf16[256,2048]{1,0:T(8,128)(2,1)}) custom-call(s32[256]{0:T(256)} %lens.3, bf16[256,2048]{1,0:T(8,128)(2,1)} %x_ref.3, f32[4,2048]{1,0:T(4,128)} %reshape.33.gain_ref, f32[4,2048]{1,0:T(4,128)} %reshape.34.bias_ref, bf16[2,768]{1,0:T(2,128)(2,1)} %reshape.35.bqkv_ref, ...), custom_call_target="tpu_custom_call" | custom-call | tf_op jit(solution)/shard_map/attention_0/pallas_call | solution.py:163
  35.4 37.0 %mlp_0.1 = (bf16[256,2048]{1,0:T(8,128)(2,1)}, bf16[2,16,2048]{2,1,0:T(8,128)(2,1)}) custom-call(bf16[256,2048]{1,0:T(8,128)(2,1)} %get-tuple-element.12.part_ref, bf16[256,2048]{1,0:T(8,128)(2,1)} %x_ref.3, f32[4,2048]{1,0:T(4,128)} %reshape.33.gain_ref, f32[4,2048]{1,0:T(4,128)} %reshape.34.bias_ref, bf16[2,2048]{1,0:T(2,128)(2,1)} %bout_ref.3, ...), custom_call_target="tpu_custom_call" | custom-call | tf_op jit(solution)/shard_map/mlp_0/pallas_call | solution.py:368
  72.5 30.5 %attention_1.1 = (bf16[2,256,256,128]{3,2,1,0:T(8,128)(2,1)}, bf16[2,256,256,128]{3,2,1,0:T(8,128)(2,1)}, bf16[256,2048]{1,0:T(8,128)(2,1)}) custom-call(s32[256]{0:T(256)} %lens.3, bf16[256,2048]{1,0:T(8,128)(2,1)} %get-tuple-element.13.x_ref, f32[4,2048]{1,0:T(4,128)} %reshape.33.gain_ref, ...), custom_call_target="tpu_custom_call", output_to_operand_aliasing={{0}: (9, {}), {1}: (10, {})} | custom-call | tf_op jit(solution)/shard_map/attention_1/pallas_call | solution.py:163
  103.0 35.4 %mlp_1.1 = (bf16[256,2048]{1,0:T(8,128)(2,1)}, bf16[8,128]{1,0:T(8,128)(2,1)}) custom-call(bf16[256,2048]{1,0:T(8,128)(2,1)} %get-tuple-element.16.part_ref, bf16[2,16,2048]{2,1,0:T(8,128)(2,1)} %get-tuple-element.17.x_ref, f32[4,2048]{1,0:T(4,128)} %reshape.33.gain_ref, f32[4,2048]{1,0:T(4,128)} %reshape.34.bias_ref, bf16[2,2048]{1,0:T(2,128)(2,1)} %bout_ref.3, ...), custom_call_target="tpu_custom_call" | custom-call | tf_op jit(solution)/shard_map/mlp_1/pallas_call | solution.py:368
  138.4 2.3 %copy.22 = bf16[256,2048]{1,0:T(8,128)(2,1)} copy(bf16[256,2048]{1,0:T(8,128)(2,1)} %get-tuple-element.24) | data formatting | bytes 2097152

commit v2 on v1

v2 whole, which is shorter than its diff:
```python
import functools

import jax
import jax.numpy as jnp
from jax import lax
from jax.experimental import pallas as pl
from jax.experimental.pallas import tpu as pltpu
from jax.sharding import PartitionSpec as P

NORM_EPS = 1e-5
MESH = pl.DeviceIdType.MESH
F32 = jnp.float32
BF16 = jnp.bfloat16
NT = (((1,), (1,)), ((), ()))
NN = (((1,), (0,)), ((), ()))

GROUP = 16
RING = 3
PIECES = 8
CHUNKS = 2


def dot(lhs, rhs, dims=NN):
    return lax.dot_general(lhs, rhs, dims, preferred_element_type=F32)


def norm(rows, gain, bias):
    mean = jnp.mean(rows, axis=-1, keepdims=True)
    centered = rows - mean
    var = jnp.mean(centered * centered, axis=-1, keepdims=True)
    return centered * lax.rsqrt(var + NORM_EPS) * gain + bias


def attention_kernel(layer, in_place, lens, x_hbm, gain_ref, bias_ref, bqkv_ref, wqkv_hbm, wout_hbm, k_in, v_in, *rest):
    if layer > 0:
        rest = rest[2:]
    ko_hbm, vo_hbm, part_ref, kbuf, vbuf, xbuf, wqkv, wout, hbuf, kcols, vcols, qbuf, qrep, sbuf, abuf, w_sem, k_sem, v_sem, ko_sem, vo_sem = rest
    batch, width = xbuf.shape
    hd = wout.shape[0]
    head = hd // 4
    slots = kbuf.shape[2]
    groups = batch // GROUP
    n = GROUP * 4
    ring = kbuf.shape[0] // GROUP

    x_copy = pltpu.make_async_copy(x_hbm, xbuf, w_sem.at[0])
    x_copy.start()
    w_copy = pltpu.make_async_copy(wqkv_hbm.at[layer], wqkv, w_sem.at[1])
    w_copy.start()

    def load(src, buf, sem, g):
        rows = pl.ds(g * GROUP, GROUP)
        return pltpu.make_async_copy(src.at[layer, rows], buf.at[rows], sem.at[g])

    def save(buf, dst, sem, g):
        rows = pl.ds(g * GROUP, GROUP)
        here = rows if in_place else pl.ds(lax.rem(g, ring) * GROUP, GROUP)
        return pltpu.make_async_copy(buf.at[here], dst.at[layer, rows], sem.at[g])

    if in_place:
        def start_loads(g, carry):
            load(k_in, kbuf, k_sem, g).start()
            load(v_in, vbuf, v_sem, g).start()
            return carry

        lax.fori_loop(0, groups, start_loads, 0)
    o_copy = pltpu.make_async_copy(wout_hbm.at[layer], wout, w_sem.at[2])
    o_copy.start()

    spread_cols = (lax.broadcasted_iota(jnp.int32, (head, hd), 0) == lax.broadcasted_iota(jnp.int32, (head, hd), 1) % head).astype(F32).astype(BF16)
    head_of = lax.broadcasted_iota(jnp.int32, (4, hd), 0) == lax.broadcasted_iota(jnp.int32, (4, hd), 1) // head

    def bias_row(part):
        wide = dot(bqkv_ref[layer, part], spread_cols)
        return jnp.sum(jnp.where(head_of, wide, 0.0), axis=0, keepdims=True)

    bias_q = bias_row(0)
    bias_kv = [jnp.broadcast_to(bias_row(part), (128, hd)).T for part in (1, 2)]

    x_copy.wait()
    if layer == 0:
        gain = gain_ref[0, 0:1, :]
        bias = bias_ref[0, 0:1, :]

        def norm_rows(i, carry):
            rows = pl.ds(i * 32, 32)
            hbuf[rows, :] = norm(xbuf[rows, :].astype(F32), gain, bias).astype(BF16)
            return carry

        lax.fori_loop(0, batch // 32, norm_rows, 0)
    else:
        hbuf = xbuf
    w_copy.wait()
    for part, pages in ((1, kcols), (2, vcols)):
        for half in range(batch // 128):
            cols = dot(wqkv[part * hd:(part + 1) * hd, :], hbuf[half * 128:(half + 1) * 128, :], NT) + bias_kv[part - 1]
            cols = cols.astype(BF16).astype(F32)
            for j in range(128 // GROUP):
                pages[half * (128 // GROUP) + j] = cols if j == 0 else pltpu.roll(cols, 128 - j * GROUP, 1)
    qbuf[...] = (dot(hbuf[...], wqkv[0:hd, :], NT) + bias_q).astype(BF16)
    own_head = lax.broadcasted_iota(jnp.int32, (n, hd), 0) % 4 == lax.broadcasted_iota(jnp.int32, (n, hd), 1) // head
    repeat = (lax.broadcasted_iota(jnp.int32, (n, GROUP), 0) // 4 == lax.broadcasted_iota(jnp.int32, (n, GROUP), 1)).astype(F32).astype(BF16)
    for g in range(groups):
        qrep[g * n:(g + 1) * n, :] = jnp.where(own_head, dot(repeat, qbuf[g * GROUP:(g + 1) * GROUP, :]), 0.0).astype(BF16)

    lane8 = lax.broadcasted_iota(jnp.int32, (8, slots), 1)
    top8 = lax.broadcasted_iota(jnp.int32, (8, slots), 0) < 4
    lane_hd = lax.broadcasted_iota(jnp.int32, (hd, slots), 1)
    scale = head ** -0.5

    def updated(src, dst, cols, g, b):
        base = g * GROUP
        column = jnp.broadcast_to(cols[:, b:b + 1], (hd, slots)).astype(BF16)
        tile = jnp.where(lane_hd == lens[base + b], column, src[base + b])
        dst[base + b if in_place else lax.rem(g, ring) * GROUP + b] = tile
        return tile

    def key_stage(g):
        base = g * GROUP
        cols = kcols[g]
        q_rows = qrep[pl.ds(pl.multiple_of(base * 4, n), n), :]
        masked = []
        for i in range(0, GROUP, 2):
            tiles = [updated(kbuf if in_place else k_in, kbuf, cols, g, b) for b in (i, i + 1)]
            both = dot(q_rows[i * 4:i * 4 + 8, :], jnp.concatenate(tiles, axis=1))
            score = jnp.where(top8, both[:, 0:slots], both[:, slots:2 * slots]) * scale
            limit = jnp.where(top8, lens[base + i], lens[base + i + 1])
            masked.append(jnp.where(lane8 <= limit, score, -1e30))
        return jnp.concatenate(masked, axis=0)

    def value_stage(g, scores):
        weights = jnp.exp(scores - jnp.max(scores, axis=-1, keepdims=True))
        prob = weights / jnp.sum(weights, axis=-1, keepdims=True)
        cols = vcols[g]
        outs = []
        for i in range(0, GROUP, 2):
            tiles = [updated(vbuf if in_place else v_in, vbuf, cols, g, b) for b in (i, i + 1)]
            pair = prob[i * 4:i * 4 + 8, :]
            spread = jnp.concatenate([jnp.where(top8, pair, 0.0), jnp.where(top8, 0.0, pair)], axis=1).astype(BF16)
            outs.append(dot(spread, jnp.concatenate(tiles, axis=1), NT))
        heads = jnp.where(own_head, jnp.concatenate(outs, axis=0), 0.0).astype(BF16)
        abuf[pl.ds(pl.multiple_of(g * n, n), n), :] = heads

    def reuse(buf, dst, sem, g):
        if not in_place:
            @pl.when(g >= ring)
            def _():
                save(buf, dst, sem, g - ring).wait()

    if in_place:
        load(k_in, kbuf, k_sem, 0).wait()
    sbuf[0] = key_stage(0)
    save(kbuf, ko_hbm, ko_sem, 0).start()

    def step(g, carry):
        if in_place:
            load(v_in, vbuf, v_sem, g - 1).wait()
            load(k_in, kbuf, k_sem, g).wait()
        reuse(kbuf, ko_hbm, ko_sem, g)
        reuse(vbuf, vo_hbm, vo_sem, g - 1)
        scores = sbuf[lax.rem(g - 1, 2)]
        sbuf[lax.rem(g, 2)] = key_stage(g)
        value_stage(g - 1, scores)
        save(kbuf, ko_hbm, ko_sem, g).start()
        save(vbuf, vo_hbm, vo_sem, g - 1).start()
        return carry

    lax.fori_loop(1, groups, step, 0)
    final = groups - 1
    if in_place:
        load(v_in, vbuf, v_sem, final).wait()
    else:
        save(vbuf, vo_hbm, vo_sem, final - ring).wait()
    value_stage(final, sbuf[final % 2])
    save(vbuf, vo_hbm, vo_sem, final).start()
    o_copy.wait()
    collect = (lax.broadcasted_iota(jnp.int32, (GROUP, n), 1) // 4 == lax.broadcasted_iota(jnp.int32, (GROUP, n), 0)).astype(F32).astype(BF16)
    for g in range(groups):
        qbuf[g * GROUP:(g + 1) * GROUP, :] = dot(collect, abuf[g * n:(g + 1) * n, :]).astype(BF16)
    for c in range(0, width, 512):
        part_ref[:, c:c + 512] = dot(qbuf[...], wout[:, c:c + 512]).astype(BF16)

    def finish(g, carry):
        save(kbuf, ko_hbm, ko_sem, g).wait()
        save(vbuf, vo_hbm, vo_sem, g).wait()
        return carry

    lax.fori_loop(0 if in_place else groups - ring, groups, finish, 0)


def attention(layer, in_place, lens, x, gains, biases, bqkv, wqkv, wout, k_in, v_in, k_out=None, v_out=None):
    batch, width = x.shape
    hd, slots = k_in.shape[-2:]
    groups = batch // GROUP
    any_spec = pl.BlockSpec(memory_space=pl.ANY)
    vmem_spec = pl.BlockSpec(memory_space=pltpu.VMEM)
    cache_spec = any_spec if in_place else vmem_spec
    args = [lens, x, gains, biases, bqkv, wqkv, wout, k_in, v_in]
    specs = [pl.BlockSpec(memory_space=pltpu.SMEM), any_spec] + [vmem_spec] * 3 + [any_spec] * 2 + [cache_spec] * 2
    alias = {}
    shape = k_in.shape
    if layer > 0:
        args += [k_out, v_out]
        specs += [any_spec] * 2
        alias = {9: 0, 10: 1}
        shape = k_out.shape
    held = batch if in_place else RING * GROUP
    dma = pltpu.SemaphoreType.DMA
    return pl.pallas_call(
        functools.partial(attention_kernel, layer, in_place),
        out_shape=(
            jax.ShapeDtypeStruct(shape, BF16),
            jax.ShapeDtypeStruct(shape, BF16),
            jax.ShapeDtypeStruct((batch, width), BF16),
        ),
        in_specs=specs,
        out_specs=(any_spec, any_spec, vmem_spec),
        input_output_aliases=alias,
        scratch_shapes=[
            pltpu.VMEM((held, hd, slots), BF16),
            pltpu.VMEM((held, hd, slots), BF16),
            pltpu.VMEM((batch, width), BF16),
            pltpu.VMEM((3 * hd, width), BF16),
            pltpu.VMEM((hd, width), BF16),
            pltpu.VMEM((batch if layer == 0 else 16, width), BF16),
            pltpu.VMEM((groups, hd, 128), F32),
            pltpu.VMEM((groups, hd, 128), F32),
            pltpu.VMEM((batch, hd), BF16),
            pltpu.VMEM((batch * 4, hd), BF16),
            pltpu.VMEM((2, GROUP * 4, slots), F32),
            pltpu.VMEM((batch * 4, hd), BF16),
            dma((3,)),
            dma((groups,)),
            dma((groups,)),
            dma((groups,)),
            dma((groups,)),
        ],
        compiler_params=pltpu.CompilerParams(vmem_limit_bytes=(60 if in_place else 24) * 1024 * 1024),
        name=f"attention_{layer}",
    )(*args)


def mlp_kernel(layer, last, part_ref, x_ref, gain_ref, bias_ref, bout_ref, bup_ref, bdown_ref, wup_hbm, wdown_hbm, *rest):
    if last:
        full_ref, rest = rest[0], rest[1:]
    else:
        k_hbm, v_hbm, full_ref, own_ref, k_next, v_next = rest[:6]
        rest = rest[6:]
    (wup, wdown, part2, hbuf, ubuf, pair_in, cross_out, cross_in, own_sum, xown,
     w_sem, pair_s, pair_r, cross_s, cross_r, gat_s, gat_r, fwd_s, fwd_r, cache_sem) = rest
    batch, width = part_ref.shape
    hidden = wup.shape[1]
    rows_c = batch // CHUNKS
    rows_o = rows_c // 8
    me = lax.axis_index("tp")
    core = lax.rem(me, 2)
    chip = lax.div(me, 2)
    cx = lax.rem(chip, 2)
    cy = lax.div(chip, 2)
    partner = chip * 2 + 1 - core
    chips = ((1 - cy) * 2 + 1 - cx, cy * 2 + 1 - cx, (1 - cy) * 2 + cx, chip)

    def device(index):
        return {"tp": index}

    def rows_of(c, owner):
        return pl.ds(pl.multiple_of(c * rows_c + owner * rows_o, rows_o), rows_o)

    copies = [
        pltpu.make_async_copy(wup_hbm.at[layer], wup, w_sem.at[0]),
        pltpu.make_async_copy(wdown_hbm.at[layer], wdown, w_sem.at[1]),
    ]
    for copy in copies:
        copy.start()
    if layer == 0:
        x_copies = [pltpu.make_async_copy(x_ref.at[rows_of(c, me)], xown.at[c], w_sem.at[2 + c]) for c in range(CHUNKS)]
        for copy in x_copies:
            copy.start()

    caches = []
    if not last:
        piece = batch // PIECES
        for p in range(PIECES):
            rows = slice(p * piece, (p + 1) * piece)
            caches.append(pltpu.make_async_copy(k_hbm.at[layer + 1, rows], k_next.at[rows], cache_sem.at[0, p]))
            caches.append(pltpu.make_async_copy(v_hbm.at[layer + 1, rows], v_next.at[rows], cache_sem.at[1, p]))
        for copy in caches:
            copy.start()

    barrier = pltpu.get_barrier_semaphore()
    for peer in (partner,) + tuple(t * 2 + core for t in chips[:3]):
        pl.semaphore_signal(barrier, inc=1, device_id=device(peer), device_id_type=MESH)
    pl.semaphore_wait(barrier, 4)

    def remote(src, dst, send, recv, target):
        return pltpu.make_async_remote_copy(
            src_ref=src, dst_ref=dst, send_sem=send, recv_sem=recv, device_id=device(target), device_id_type=MESH)

    def pair_copy(s, c, k):
        src = part_ref if s == 0 else part2
        return remote(src.at[rows_of(c, chips[k] * 2 + 1 - core)], pair_in.at[s, c, k],
                      pair_s.at[s, c, k], pair_r.at[s, c, k], partner)

    def cross_copy(s, c, k):
        return remote(cross_out.at[s, c, k], cross_in.at[s, c, k],
                      cross_s.at[s, c, k], cross_r.at[s, c, k], chips[k] * 2 + core)

    def gather_copy(s, c, k):
        rows = rows_of(c, me)
        target = partner if k == 3 else chips[k] * 2 + core
        return remote(hbuf.at[s, rows], hbuf.at[s, rows], gat_s.at[s, c, k], gat_r.at[s, c, k], target)

    def forward_copy(s, c, k):
        rows = rows_of(c, chips[k] * 2 + core)
        return remote(hbuf.at[s, rows], hbuf.at[s, rows], fwd_s.at[s, c, k], fwd_r.at[s, c, k], partner)

    def send_pairs(s, c):
        for k in range(4):
            pair_copy(s, c, k).start()

    def add_pairs(s, c):
        src = part_ref if s == 0 else part2
        for k in range(4):
            pair_copy(s, c, k).wait_recv()
            both = src[rows_of(c, chips[k] * 2 + core), :].astype(F32) + pair_in[s, c, k].astype(F32)
            if k < 3:
                cross_out[s, c, k] = both.astype(BF16)
                cross_copy(s, c, k).start()
            else:
                own_sum[c] = both

    def own_total(s, c):
        total = own_sum[c]
        for k in (1, 2, 0):
            cross_copy(s, c, k).wait_recv()
            total = total + cross_in[s, c, k].astype(F32)
        return total

    def send_own(s, c):
        for k in range(4):
            gather_copy(s, c, k).start()

    def forward(s, c):
        for k in (1, 2, 0):
            gather_copy(s, c, k).wait_recv()
            forward_copy(s, c, k).start()

    def arrived(s, c):
        gather_copy(s, c, 3).wait_recv()
        for k in range(3):
            forward_copy(s, c, k).wait_recv()

    def row(ref, index):
        return ref[index:index + 1, :].astype(F32)

    def first_finish(c):
        total = own_total(0, c)
        old = xown[c] if layer == 0 else x_ref[c]
        mid = (old.astype(F32) + total + row(bout_ref, layer)).astype(BF16)
        xown[c] = mid
        hbuf[0, rows_of(c, me), :] = norm(mid.astype(F32), gain_ref[layer, 1:2, :], bias_ref[layer, 1:2, :]).astype(BF16)
        send_own(0, c)

    def second_finish(c):
        total = own_total(1, c)
        new = (xown[c].astype(F32) + total + row(bdown_ref, layer)).astype(BF16)
        if last:
            hbuf[1, rows_of(c, me), :] = new
        else:
            own_ref[c] = new
            hbuf[1, rows_of(c, me), :] = norm(new.astype(F32), gain_ref[layer + 1, 0:1, :], bias_ref[layer + 1, 0:1, :]).astype(BF16)
        send_own(1, c)

    def mlp(c):
        rows = slice(c * rows_c, (c + 1) * rows_c)
        h = hbuf[0, rows, :]
        for n in range(0, hidden, 256):
            up = dot(h, wup[:, n:n + 256]) + bup_ref[layer:layer + 1, n:n + 256].astype(F32)
            ubuf[:, n:n + 256] = jnp.maximum(up, 0.0).astype(BF16)
        u = ubuf[...]
        for n in range(0, width, 256):
            part2[rows, n:n + 256] = dot(u, wdown[:, n:n + 256]).astype(BF16)

    for c in range(CHUNKS):
        send_pairs(0, c)
    for c in range(CHUNKS):
        add_pairs(0, c)
    if layer == 0:
        for copy in x_copies:
            copy.wait()
    for c in range(CHUNKS):
        first_finish(c)
    for copy in copies:
        copy.wait()
    for c in range(CHUNKS):
        forward(0, c)
        if c > 0:
            add_pairs(1, c - 1)
        arrived(0, c)
        mlp(c)
        send_pairs(1, c)
    add_pairs(1, CHUNKS - 1)
    for c in range(CHUNKS):
        second_finish(c)
    for c in range(CHUNKS):
        forward(1, c)
    for c in range(CHUNKS):
        arrived(1, c)
        rows = slice(c * rows_c, (c + 1) * rows_c)
        full_ref[rows, :] = hbuf[1, rows, :]
    for copy in caches:
        copy.wait()
    for s in range(2):
        for c in range(CHUNKS):
            for k in range(4):
                pair_copy(s, c, k).wait_send()
                gather_copy(s, c, k).wait_send()
                if k < 3:
                    cross_copy(s, c, k).wait_send()
                    forward_copy(s, c, k).wait_send()


def mlp_block(layer, last, part, x, gains, biases, bout, bup, bdown, wup, wdown, k_in, v_in):
    batch, width = part.shape
    hidden = wup.shape[2]
    rows_o = batch // CHUNKS // 8
    any_spec = pl.BlockSpec(memory_space=pl.ANY)
    vmem_spec = pl.BlockSpec(memory_space=pltpu.VMEM)
    own = (CHUNKS, rows_o, width)
    args = [part, x, gains, biases, bout, bup, bdown, wup, wdown]
    in_specs = [vmem_spec, any_spec if layer == 0 else vmem_spec] + [vmem_spec] * 5 + [any_spec] * 2
    out_shape = [jax.ShapeDtypeStruct((batch, width), BF16)]
    if not last:
        args += [k_in, v_in]
        in_specs += [any_spec] * 2
        out_shape += [jax.ShapeDtypeStruct(own, BF16), pltpu.VMEM(k_in.shape[1:], BF16), pltpu.VMEM(v_in.shape[1:], BF16)]
    dma = pltpu.SemaphoreType.DMA
    return pl.pallas_call(
        functools.partial(mlp_kernel, layer, last),
        out_shape=out_shape,
        in_specs=in_specs,
        out_specs=[vmem_spec] * len(out_shape),
        scratch_shapes=[
            pltpu.VMEM((width, hidden), BF16),
            pltpu.VMEM((hidden, width), BF16),
            pltpu.VMEM((batch, width), BF16),
            pltpu.VMEM((2, batch, width), BF16),
            pltpu.VMEM((batch // CHUNKS, hidden), BF16),
            pltpu.VMEM((2, CHUNKS, 4, rows_o, width), BF16),
            pltpu.VMEM((2, CHUNKS, 3, rows_o, width), BF16),
            pltpu.VMEM((2, CHUNKS, 3, rows_o, width), BF16),
            pltpu.VMEM(own, F32),
            pltpu.VMEM(own, BF16),
            dma((2 + CHUNKS,)),
            dma((2, CHUNKS, 4)),
            dma((2, CHUNKS, 4)),
            dma((2, CHUNKS, 3)),
            dma((2, CHUNKS, 3)),
            dma((2, CHUNKS, 4)),
            dma((2, CHUNKS, 4)),
            dma((2, CHUNKS, 3)),
            dma((2, CHUNKS, 3)),
            dma((2, PIECES)),
        ],
        compiler_params=pltpu.CompilerParams(
            collective_id=layer, has_side_effects=True, vmem_limit_bytes=(60 if last else 24) * 1024 * 1024),
        name=f"mlp_{layer}",
    )(*args)


def solution(mesh):
    cache_spec = P(None, 'dp', 'tp', None, None)
    in_specs = (P('dp', None), P('dp'), cache_spec, cache_spec, P(), P(),
                P(None, None, None, 'tp', None), P(None, None, 'tp', None),
                P(None, 'tp', None, None), P(), P(None, None, 'tp'), P(None, 'tp'),
                P(None, 'tp', None), P())
    out_specs = (P('dp', None), cache_spec, cache_spec)

    def local_step(x, cache_len, k_cache, v_cache, norm_gain, norm_bias, w_qkv, b_qkv, w_out, b_out, w_up, b_up, w_down, b_down):
        layers, batch, heads, slots, head = k_cache.shape
        width = x.shape[1]
        hd = heads * head
        k_in = jnp.swapaxes(k_cache, 3, 4).reshape(layers, batch, hd, slots)
        v_in = jnp.swapaxes(v_cache, 3, 4).reshape(layers, batch, hd, slots)
        wqkv = jnp.transpose(w_qkv, (0, 2, 3, 4, 1)).reshape(layers, 3 * hd, width)
        wout = w_out.reshape(layers, hd, width)

        rows, own = x, x
        caches = (k_in, v_in)
        for layer in range(layers):
            k_out, v_out, part = attention(layer, layer == 0, cache_len, rows, norm_gain, norm_bias, b_qkv, wqkv, wout, *caches)
            last = layer == layers - 1
            rows, *held = mlp_block(layer, last, part, own, norm_gain, norm_bias, b_out, b_up, b_down, w_up, w_down, k_in, v_in)
            if not last:
                own, k_next, v_next = held
                caches = (pltpu.with_memory_space_constraint(k_next, pltpu.VMEM), pltpu.with_memory_space_constraint(v_next, pltpu.VMEM), k_out, v_out)

        def back(cache):
            return jnp.swapaxes(cache.reshape(layers, batch, heads, head, slots), 3, 4)

        return rows, back(k_out), back(v_out)

    return jax.shard_map(local_step, mesh=mesh, in_specs=in_specs, out_specs=out_specs, check_vma=False)
```

time: 141 us -> 130 us (0.922)
  Pallas kernels: 134 us -> 126 us
  local copies, waits for them, and re-layouts: 6.45 us -> 2.3 us
    pallas_call x4, Pallas kernels: 134 us -> 126 us  [the longest x2 77.7 us: mlp_block(): pl.pallas_call(functools.partial(mlp_kernel, layer, last), out_shape=out_...]
    reshape x3 -> x0, local copies, waits for them, and re-layouts: 4.15 us -> none  [the longest x1 1.4 us: local_step(): biases = norm_bias.reshape(2 * layers, width)]
where the time goes in v2:
time: 130 us; the launch traced here: 129 us
  Pallas kernels  126 us (97%)
  local copies, waits for them, and re-layouts  2.3 us (2%)
    pallas_call x2, Pallas kernels, mlp_block(): pl.pallas_call(functools.partial(mlp_kernel, layer, last), out_shape=out_...  77.7 us
    pallas_call x2, Pallas kernels, attention(): pl.pallas_call(functools.partial(attention_kernel, layer, in_place), out_...  48.5 us

profile of v2, /device:TPU:0, one launch (start us, length us, event | category | flops | bytes accessed | tf_op | source)
XLA Modules:
  0.0 129.2 jit_solution(12656857970957299774)
XLA Ops:
  0.6 25.9 %attention_0.1 = (bf16[2,256,256,128]{3,2,1,0:T(8,128)(2,1)}, bf16[2,256,256,128]{3,2,1,0:T(8,128)(2,1)}, bf16[256,2048]{1,0:T(8,128)(2,1)}) custom-call(s32[256]{0:T(256)} %lens.3, bf16[256,2048]{1,0:T(8,128)(2,1)} %x_ref.1, f32[2,2,2048]{2,1,0:T(2,128)} %gain_ref.7, f32[2,2,2048]{2,1,0:T(2,128)} %bias_ref.7, bf16[2,3,4,64]{3,2,1,0:T(4,128)(2,1)} %bqkv_ref.3, ...), custom_call_target="tpu_custom_call" | custom-call | tf_op jit(solution)/shard_map/attention_0/pallas_call | solution.py:209
  26.5 42.2 %mlp_0.1 = (bf16[256,2048]{1,0:T(8,128)(2,1)}, bf16[2,16,2048]{2,1,0:T(8,128)(2,1)}, bf16[256,256,128]{2,1,0:T(8,128)(2,1)S(1)}, bf16[256,256,128]{2,1,0:T(8,128)(2,1)S(1)}) custom-call(bf16[256,2048]{1,0:T(8,128)(2,1)} %get-tuple-element.13.part_ref, bf16[256,2048]{1,0:T(8,128)(2,1)} %x_ref.1, f32[2,2,2048]{2,1,0:T(2,128)} %gain_ref.7, ...), custom_call_target="tpu_custom_call" | custom-call | tf_op jit(solution)/shard_map/mlp_0/pallas_call | solution.py:438
  68.7 22.7 %attention_1.1 = (bf16[2,256,256,128]{3,2,1,0:T(8,128)(2,1)}, bf16[2,256,256,128]{3,2,1,0:T(8,128)(2,1)}, bf16[256,2048]{1,0:T(8,128)(2,1)}) custom-call(s32[256]{0:T(256)} %lens.3, bf16[256,2048]{1,0:T(8,128)(2,1)} %get-tuple-element.14.x_hbm, f32[2,2,2048]{2,1,0:T(2,128)} %gain_ref.7, ...), custom_call_target="tpu_custom_call", output_to_operand_aliasing={{0}: (9, {}), {1}: (10, {})} | custom-call | tf_op jit(solution)/shard_map/attention_1/pallas_call | solution.py:209
  91.4 35.6 %mlp_1.1 = bf16[256,2048]{1,0:T(8,128)(2,1)} custom-call(bf16[256,2048]{1,0:T(8,128)(2,1)} %get-tuple-element.19.part_ref, bf16[2,16,2048]{2,1,0:T(8,128)(2,1)} %get-tuple-element.20.x_ref, f32[2,2,2048]{2,1,0:T(2,128)} %gain_ref.7, f32[2,2,2048]{2,1,0:T(2,128)} %bias_ref.7, bf16[2,2048]{1,0:T(2,128)(2,1)} %bout_ref.3, bf16[2,1024]{1,0:T(2,128)(2,1)} %bup_ref.3, ...), custom_call_target="tpu_custom_call" | custom-call | tf_op jit(solution)/shard_map/mlp_1/pallas_call | solution.py:438
  126.9 2.3 %copy.22 = bf16[256,2048]{1,0:T(8,128)(2,1)} copy(bf16[256,2048]{1,0:T(8,128)(2,1)} %mlp_1.1) | data formatting | bytes 2097152

commit v3 on v2

--- a/solution.py
+++ b/solution.py
@@ -31,11 +31,15 @@
     return centered * lax.rsqrt(var + NORM_EPS) * gain + bias
 
 
-def attention_kernel(layer, in_place, lens, x_hbm, gain_ref, bias_ref, bqkv_ref, wqkv_hbm, wout_hbm, k_in, v_in, *rest):
+def attention_kernel(layer, fetch, lens, x_hbm, gain_ref, bias_ref, bqkv_ref, wqkv_hbm, wout_hbm, k_in, v_in, *rest):
     if layer > 0:
         rest = rest[2:]
+    if fetch:
+        k_hbm, v_hbm = k_in, v_in
+        k_in, v_in = rest[-2:]
+        rest = rest[:-2]
     ko_hbm, vo_hbm, part_ref, kbuf, vbuf, xbuf, wqkv, wout, hbuf, kcols, vcols, qbuf, qrep, sbuf, abuf, w_sem, k_sem, v_sem, ko_sem, vo_sem = rest
-    batch, width = xbuf.shape
+    batch, width = x_hbm.shape
     hd = wout.shape[0]
     head = hd // 4
     slots = kbuf.shape[2]
@@ -54,13 +58,13 @@
 
     def save(buf, dst, sem, g):
         rows = pl.ds(g * GROUP, GROUP)
-        here = rows if in_place else pl.ds(lax.rem(g, ring) * GROUP, GROUP)
+        here = pl.ds(lax.rem(g, ring) * GROUP, GROUP)
         return pltpu.make_async_copy(buf.at[here], dst.at[layer, rows], sem.at[g])
 
-    if in_place:
+    if fetch:
         def start_loads(g, carry):
-            load(k_in, kbuf, k_sem, g).start()
-            load(v_in, vbuf, v_sem, g).start()
+            load(k_hbm, k_in, k_sem, g).start()
+            load(v_hbm, v_in, v_sem, g).start()
             return carry
 
         lax.fori_loop(0, groups, start_loads, 0)
@@ -93,10 +97,8 @@
     w_copy.wait()
     for part, pages in ((1, kcols), (2, vcols)):
         for half in range(batch // 128):
-            cols = dot(wqkv[part * hd:(part + 1) * hd, :], hbuf[half * 128:(half + 1) * 128, :], NT) + bias_kv[part - 1]
-            cols = cols.astype(BF16).astype(F32)
-            for j in range(128 // GROUP):
-                pages[half * (128 // GROUP) + j] = cols if j == 0 else pltpu.roll(cols, 128 - j * GROUP, 1)
+            cols = dot(wqkv[part * hd:(part + 1) * hd, :], hbuf[half * 128:(half + 1) * 128, :], NT)
+            pages[half] = (cols + bias_kv[part - 1]).astype(BF16)
     qbuf[...] = (dot(hbuf[...], wqkv[0:hd, :], NT) + bias_q).astype(BF16)
     own_head = lax.broadcasted_iota(jnp.int32, (n, hd), 0) % 4 == lax.broadcasted_iota(jnp.int32, (n, hd), 1) // head
     repeat = (lax.broadcasted_iota(jnp.int32, (n, GROUP), 0) // 4 == lax.broadcasted_iota(jnp.int32, (n, GROUP), 1)).astype(F32).astype(BF16)
@@ -105,73 +107,79 @@
 
     lane8 = lax.broadcasted_iota(jnp.int32, (8, slots), 1)
     top8 = lax.broadcasted_iota(jnp.int32, (8, slots), 0) < 4
-    lane_hd = lax.broadcasted_iota(jnp.int32, (hd, slots), 1)
+    lane16 = lax.broadcasted_iota(jnp.int32, (16, slots), 1).astype(F32).astype(BF16)
     scale = head ** -0.5
 
     def updated(src, dst, cols, g, b):
         base = g * GROUP
-        column = jnp.broadcast_to(cols[:, b:b + 1], (hd, slots)).astype(BF16)
-        tile = jnp.where(lane_hd == lens[base + b], column, src[base + b])
-        dst[base + b if in_place else lax.rem(g, ring) * GROUP + b] = tile
+        column = pltpu.roll(cols, (lens[base + b] - base - b) & (slots - 1), 1).reshape(hd // 16, 16, slots)
+        here = lane16 == jnp.full((16, slots), lens[base + b].astype(F32), F32).astype(BF16)
+        tile = jnp.where(here[None], column, src[base + b].reshape(hd // 16, 16, slots)).reshape(hd, slots)
+        dst[lax.rem(g, ring) * GROUP + b] = tile
         return tile
 
-    def key_stage(g):
+    def key_pair(g, i, cols, q_rows):
         base = g * GROUP
-        cols = kcols[g]
-        q_rows = qrep[pl.ds(pl.multiple_of(base * 4, n), n), :]
-        masked = []
+        tiles = [updated(k_in, kbuf, cols, g, b) for b in (i, i + 1)]
+        both = dot(q_rows[i * 4:i * 4 + 8, :], jnp.concatenate(tiles, axis=1))
+        score = jnp.where(top8, both[:, 0:slots], both[:, slots:2 * slots]) * scale
+        limit = jnp.where(top8, lens[base + i], lens[base + i + 1])
+        return jnp.where(lane8 <= limit, score, -1e30)
+
+    def value_pair(g, i, cols, prob):
+        tiles = [updated(v_in, vbuf, cols, g, b) for b in (i, i + 1)]
+        pair = prob[i * 4:i * 4 + 8, :]
+        spread = jnp.concatenate([jnp.where(top8, pair, 0.0), jnp.where(top8, 0.0, pair)], axis=1).astype(BF16)
+        return dot(spread, jnp.concatenate(tiles, axis=1), NT)
+
+    def stage(key_group, value_group):
+        if value_group is not None:
+            scores = sbuf[lax.rem(value_group, 2)]
+            weights = jnp.exp(scores - jnp.max(scores, axis=-1, keepdims=True))
+            prob = weights / jnp.sum(weights, axis=-1, keepdims=True)
+            v_cols = vcols[lax.div(value_group, 128 // GROUP)]
+        if key_group is not None:
+            k_cols = kcols[lax.div(key_group, 128 // GROUP)]
+            q_rows = qrep[pl.ds(pl.multiple_of(key_group * n, n), n), :]
+        masked, outs = [], []
         for i in range(0, GROUP, 2):
-            tiles = [updated(kbuf if in_place else k_in, kbuf, cols, g, b) for b in (i, i + 1)]
-            both = dot(q_rows[i * 4:i * 4 + 8, :], jnp.concatenate(tiles, axis=1))
-            score = jnp.where(top8, both[:, 0:slots], both[:, slots:2 * slots]) * scale
-            limit = jnp.where(top8, lens[base + i], lens[base + i + 1])
-            masked.append(jnp.where(lane8 <= limit, score, -1e30))
-        return jnp.concatenate(masked, axis=0)
-
-    def value_stage(g, scores):
-        weights = jnp.exp(scores - jnp.max(scores, axis=-1, keepdims=True))
-        prob = weights / jnp.sum(weights, axis=-1, keepdims=True)
-        cols = vcols[g]
-        outs = []
-        for i in range(0, GROUP, 2):
-            tiles = [updated(vbuf if in_place else v_in, vbuf, cols, g, b) for b in (i, i + 1)]
-            pair = prob[i * 4:i * 4 + 8, :]
-            spread = jnp.concatenate([jnp.where(top8, pair, 0.0), jnp.where(top8, 0.0, pair)], axis=1).astype(BF16)
-            outs.append(dot(spread, jnp.concatenate(tiles, axis=1), NT))
-        heads = jnp.where(own_head, jnp.concatenate(outs, axis=0), 0.0).astype(BF16)
-        abuf[pl.ds(pl.multiple_of(g * n, n), n), :] = heads
+            if key_group is not None:
+                masked.append(key_pair(key_group, i, k_cols, q_rows))
+            if value_group is not None:
+                outs.append(value_pair(value_group, i, v_cols, prob))
+        if key_group is not None:
+            sbuf[lax.rem(key_group, 2)] = jnp.concatenate(masked, axis=0)
+        if value_group is not None:
+            heads = jnp.where(own_head, jnp.concatenate(outs, axis=0), 0.0).astype(BF16)
+            abuf[pl.ds(pl.multiple_of(value_group * n, n), n), :] = heads
 
     def reuse(buf, dst, sem, g):
-        if not in_place:
-            @pl.when(g >= ring)
-            def _():
-                save(buf, dst, sem, g - ring).wait()
-
-    if in_place:
-        load(k_in, kbuf, k_sem, 0).wait()
-    sbuf[0] = key_stage(0)
+        @pl.when(g >= ring)
+        def _():
+            save(buf, dst, sem, g - ring).wait()
+
+    if fetch:
+        load(k_hbm, k_in, k_sem, 0).wait()
+    stage(jnp.int32(0), None)
     save(kbuf, ko_hbm, ko_sem, 0).start()
 
     def step(g, carry):
-        if in_place:
-            load(v_in, vbuf, v_sem, g - 1).wait()
-            load(k_in, kbuf, k_sem, g).wait()
+        if fetch:
+            load(v_hbm, v_in, v_sem, g - 1).wait()
+            load(k_hbm, k_in, k_sem, g).wait()
         reuse(kbuf, ko_hbm, ko_sem, g)
         reuse(vbuf, vo_hbm, vo_sem, g - 1)
-        scores = sbuf[lax.rem(g - 1, 2)]
-        sbuf[lax.rem(g, 2)] = key_stage(g)
-        value_stage(g - 1, scores)
+        stage(g, g - 1)
         save(kbuf, ko_hbm, ko_sem, g).start()
         save(vbuf, vo_hbm, vo_sem, g - 1).start()
         return carry
 
     lax.fori_loop(1, groups, step, 0)
     final = groups - 1
-    if in_place:
-        load(v_in, vbuf, v_sem, final).wait()
-    else:
-        save(vbuf, vo_hbm, vo_sem, final - ring).wait()
-    value_stage(final, sbuf[final % 2])
+    if fetch:
+        load(v_hbm, v_in, v_sem, final).wait()
+    save(vbuf, vo_hbm, vo_sem, final - ring).wait()
+    stage(None, jnp.int32(final))
     save(vbuf, vo_hbm, vo_sem, final).start()
     o_copy.wait()
     collect = (lax.broadcasted_iota(jnp.int32, (GROUP, n), 1) // 4 == lax.broadcasted_iota(jnp.int32, (GROUP, n), 0)).astype(F32).astype(BF16)
@@ -185,16 +193,16 @@
         save(vbuf, vo_hbm, vo_sem, g).wait()
         return carry
 
-    lax.fori_loop(0 if in_place else groups - ring, groups, finish, 0)
-
-
-def attention(layer, in_place, lens, x, gains, biases, bqkv, wqkv, wout, k_in, v_in, k_out=None, v_out=None):
+    lax.fori_loop(groups - ring, groups, finish, 0)
+
+
+def attention(layer, fetch, lens, x, gains, biases, bqkv, wqkv, wout, k_in, v_in, k_out=None, v_out=None):
     batch, width = x.shape
     hd, slots = k_in.shape[-2:]
     groups = batch // GROUP
     any_spec = pl.BlockSpec(memory_space=pl.ANY)
     vmem_spec = pl.BlockSpec(memory_space=pltpu.VMEM)
-    cache_spec = any_spec if in_place else vmem_spec
+    cache_spec = any_spec if fetch else vmem_spec
     args = [lens, x, gains, biases, bqkv, wqkv, wout, k_in, v_in]
     specs = [pl.BlockSpec(memory_space=pltpu.SMEM), any_spec] + [vmem_spec] * 3 + [any_spec] * 2 + [cache_spec] * 2
     alias = {}
@@ -204,10 +212,11 @@
         specs += [any_spec] * 2
         alias = {9: 0, 10: 1}
         shape = k_out.shape
-    held = batch if in_place else RING * GROUP
+    held = RING * GROUP
+    fetched = [pltpu.VMEM((batch, hd, slots), BF16)] * 2 if fetch else []
     dma = pltpu.SemaphoreType.DMA
     return pl.pallas_call(
-        functools.partial(attention_kernel, layer, in_place),
+        functools.partial(attention_kernel, layer, fetch),
         out_shape=(
             jax.ShapeDtypeStruct(shape, BF16),
             jax.ShapeDtypeStruct(shape, BF16),
@@ -223,8 +232,8 @@
             pltpu.VMEM((3 * hd, width), BF16),
             pltpu.VMEM((hd, width), BF16),
             pltpu.VMEM((batch if layer == 0 else 16, width), BF16),
-            pltpu.VMEM((groups, hd, 128), F32),
-            pltpu.VMEM((groups, hd, 128), F32),
+            pltpu.VMEM((batch // 128, hd, 128), BF16),
+            pltpu.VMEM((batch // 128, hd, 128), BF16),
             pltpu.VMEM((batch, hd), BF16),
             pltpu.VMEM((batch * 4, hd), BF16),
             pltpu.VMEM((2, GROUP * 4, slots), F32),
@@ -234,10 +243,14 @@
             dma((groups,)),
             dma((groups,)),
             dma((groups,)),
-        ],
-        compiler_params=pltpu.CompilerParams(vmem_limit_bytes=(60 if in_place else 24) * 1024 * 1024),
+        ] + fetched,
+        compiler_params=pltpu.CompilerParams(vmem_limit_bytes=(60 if fetch else 24) * 1024 * 1024),
         name=f"attention_{layer}",
     )(*args)
+
+
+def in_vmem(array):
+    return pltpu.with_memory_space_constraint(array, pltpu.VMEM)
 
 
 def mlp_kernel(layer, last, part_ref, x_ref, gain_ref, bias_ref, bout_ref, bup_ref, bdown_ref, wup_hbm, wdown_hbm, *rest):
@@ -266,6 +279,102 @@
     def rows_of(c, owner):
         return pl.ds(pl.multiple_of(c * rows_c + owner * rows_o, rows_o), rows_o)
 
+    barrier = pltpu.get_barrier_semaphore()
+    for peer in (partner,) + tuple(t * 2 + core for t in chips[:3]):
+        pl.semaphore_signal(barrier, inc=1, device_id=device(peer), device_id_type=MESH)
+    pl.semaphore_wait(barrier, 4)
+
+    def remote(src, dst, send, recv, target):
+        return pltpu.make_async_remote_copy(
+            src_ref=src, dst_ref=dst, send_sem=send, recv_sem=recv, device_id=device(target), device_id_type=MESH)
+
+    def pair_copy(s, c, k):
+        src = part_ref if s == 0 else part2
+        return remote(src.at[rows_of(c, chips[k] * 2 + 1 - core)], pair_in.at[s, c, k],
+                      pair_s.at[s, c, k], pair_r.at[s, c, k], partner)
+
+    def cross_copy(s, c, k):
+        return remote(cross_out.at[s, c, k], cross_in.at[s, c, k],
+                      cross_s.at[s, c, k], cross_r.at[s, c, k], chips[k] * 2 + core)
+
+    def gather_copy(s, c, k):
+        rows = rows_of(c, me)
+        target = partner if k == 3 else chips[k] * 2 + core
+        return remote(hbuf.at[s, rows], hbuf.at[s, rows], gat_s.at[s, c, k], gat_r.at[s, c, k], target)
+
+    def forward_copy(s, c, k):
+        rows = rows_of(c, chips[k] * 2 + core)
+        return remote(hbuf.at[s, rows], hbuf.at[s, rows], fwd_s.at[s, c, k], fwd_r.at[s, c, k], partner)
+
+    def send_pairs(s, c):
+        for k in range(4):
+            pair_copy(s, c, k).start()
+
+    def add_pairs(s, c):
+        src = part_ref if s == 0 else part2
+        for k in range(4):
+            pair_copy(s, c, k).wait_recv()
+            both = src[rows_of(c, chips[k] * 2 + core), :].astype(F32) + pair_in[s, c, k].astype(F32)
+            if k < 3:
+                cross_out[s, c, k] = both.astype(BF16)
+                cross_copy(s, c, k).start()
+            else:
+                own_sum[c] = both
+
+    def own_total(s, c):
+        total = own_sum[c]
+        for k in (1, 2, 0):
+            cross_copy(s, c, k).wait_recv()
+            total = total + cross_in[s, c, k].astype(F32)
+        return total
+
+    def send_own(s, c):
+        for k in range(4):
+            gather_copy(s, c, k).start()
+
+    def forward(s, c):
+        for k in (1, 2, 0):
+            gather_copy(s, c, k).wait_recv()
+            forward_copy(s, c, k).start()
+
+    def arrived(s, c):
+        gather_copy(s, c, 3).wait_recv()
+        for k in range(3):
+            forward_copy(s, c, k).wait_recv()
+
+    def row(ref, index):
+        return ref[index:index + 1, :].astype(F32)
+
+    def first_finish(c):
+        total = own_total(0, c)
+        old = xown[c] if layer == 0 else x_ref[c]
+        mid = (old.astype(F32) + total + row(bout_ref, layer)).astype(BF16)
+        xown[c] = mid
+        hbuf[0, rows_of(c, me), :] = norm(mid.astype(F32), gain_ref[layer, 1:2, :], bias_ref[layer, 1:2, :]).astype(BF16)
+        send_own(0, c)
+
+    def second_finish(c):
+        total = own_total(1, c)
+        new = (xown[c].astype(F32) + total + row(bdown_ref, layer)).astype(BF16)
+        if last:
+            hbuf[1, rows_of(c, me), :] = new
+        else:
+            own_ref[c] = new
+            hbuf[1, rows_of(c, me), :] = norm(new.astype(F32), gain_ref[layer + 1, 0:1, :], bias_ref[layer + 1, 0:1, :]).astype(BF16)
+        send_own(1, c)
+
+    def mlp(c):
+        rows = slice(c * rows_c, (c + 1) * rows_c)
+        h = hbuf[0, rows, :]
+        for n in range(0, hidden, 256):
+            up = dot(h, wup[:, n:n + 256]) + bup_ref[layer:layer + 1, n:n + 256].astype(F32)
+            ubuf[:, n:n + 256] = jnp.maximum(up, 0.0).astype(BF16)
+        u = ubuf[...]
+        for n in range(0, width, 256):
+            part2[rows, n:n + 256] = dot(u, wdown[:, n:n + 256]).astype(BF16)
+
+    for c in range(CHUNKS):
+        send_pairs(0, c)
     copies = [
         pltpu.make_async_copy(wup_hbm.at[layer], wup, w_sem.at[0]),
         pltpu.make_async_copy(wdown_hbm.at[layer], wdown, w_sem.at[1]),
@@ -284,112 +393,22 @@
             rows = slice(p * piece, (p + 1) * piece)
             caches.append(pltpu.make_async_copy(k_hbm.at[layer + 1, rows], k_next.at[rows], cache_sem.at[0, p]))
             caches.append(pltpu.make_async_copy(v_hbm.at[layer + 1, rows], v_next.at[rows], cache_sem.at[1, p]))
-        for copy in caches:
+    started = []
+
+    def start_caches(count):
+        for copy in caches[len(started):len(started) + count]:
             copy.start()
-
-    barrier = pltpu.get_barrier_semaphore()
-    for peer in (partner,) + tuple(t * 2 + core for t in chips[:3]):
-        pl.semaphore_signal(barrier, inc=1, device_id=device(peer), device_id_type=MESH)
-    pl.semaphore_wait(barrier, 4)
-
-    def remote(src, dst, send, recv, target):
-        return pltpu.make_async_remote_copy(
-            src_ref=src, dst_ref=dst, send_sem=send, recv_sem=recv, device_id=device(target), device_id_type=MESH)
-
-    def pair_copy(s, c, k):
-        src = part_ref if s == 0 else part2
-        return remote(src.at[rows_of(c, chips[k] * 2 + 1 - core)], pair_in.at[s, c, k],
-                      pair_s.at[s, c, k], pair_r.at[s, c, k], partner)
-
-    def cross_copy(s, c, k):
-        return remote(cross_out.at[s, c, k], cross_in.at[s, c, k],
-                      cross_s.at[s, c, k], cross_r.at[s, c, k], chips[k] * 2 + core)
-
-    def gather_copy(s, c, k):
-        rows = rows_of(c, me)
-        target = partner if k == 3 else chips[k] * 2 + core
-        return remote(hbuf.at[s, rows], hbuf.at[s, rows], gat_s.at[s, c, k], gat_r.at[s, c, k], target)
-
-    def forward_copy(s, c, k):
-        rows = rows_of(c, chips[k] * 2 + core)
-        return remote(hbuf.at[s, rows], hbuf.at[s, rows], fwd_s.at[s, c, k], fwd_r.at[s, c, k], partner)
-
-    def send_pairs(s, c):
-        for k in range(4):
-            pair_copy(s, c, k).start()
-
-    def add_pairs(s, c):
-        src = part_ref if s == 0 else part2
-        for k in range(4):
-            pair_copy(s, c, k).wait_recv()
-            both = src[rows_of(c, chips[k] * 2 + core), :].astype(F32) + pair_in[s, c, k].astype(F32)
-            if k < 3:
-                cross_out[s, c, k] = both.astype(BF16)
-                cross_copy(s, c, k).start()
-            else:
-                own_sum[c] = both
-
-    def own_total(s, c):
-        total = own_sum[c]
-        for k in (1, 2, 0):
-            cross_copy(s, c, k).wait_recv()
-            total = total + cross_in[s, c, k].astype(F32)
-        return total
-
-    def send_own(s, c):
-        for k in range(4):
-            gather_copy(s, c, k).start()
-
-    def forward(s, c):
-        for k in (1, 2, 0):
-            gather_copy(s, c, k).wait_recv()
-            forward_copy(s, c, k).start()
-
-    def arrived(s, c):
-        gather_copy(s, c, 3).wait_recv()
-        for k in range(3):
-            forward_copy(s, c, k).wait_recv()
-
-    def row(ref, index):
-        return ref[index:index + 1, :].astype(F32)
-
-    def first_finish(c):
-        total = own_total(0, c)
-        old = xown[c] if layer == 0 else x_ref[c]
-        mid = (old.astype(F32) + total + row(bout_ref, layer)).astype(BF16)
-        xown[c] = mid
-        hbuf[0, rows_of(c, me), :] = norm(mid.astype(F32), gain_ref[layer, 1:2, :], bias_ref[layer, 1:2, :]).astype(BF16)
-        send_own(0, c)
-
-    def second_finish(c):
-        total = own_total(1, c)
-        new = (xown[c].astype(F32) + total + row(bdown_ref, layer)).astype(BF16)
-        if last:
-            hbuf[1, rows_of(c, me), :] = new
-        else:
-            own_ref[c] = new
-            hbuf[1, rows_of(c, me), :] = norm(new.astype(F32), gain_ref[layer + 1, 0:1, :], bias_ref[layer + 1, 0:1, :]).astype(BF16)
-        send_own(1, c)
-
-    def mlp(c):
-        rows = slice(c * rows_c, (c + 1) * rows_c)
-        h = hbuf[0, rows, :]
-        for n in range(0, hidden, 256):
-            up = dot(h, wup[:, n:n + 256]) + bup_ref[layer:layer + 1, n:n + 256].astype(F32)
-            ubuf[:, n:n + 256] = jnp.maximum(up, 0.0).astype(BF16)
-        u = ubuf[...]
-        for n in range(0, width, 256):
-            part2[rows, n:n + 256] = dot(u, wdown[:, n:n + 256]).astype(BF16)
-
-    for c in range(CHUNKS):
-        send_pairs(0, c)
+            started.append(copy)
+
     for c in range(CHUNKS):
         add_pairs(0, c)
+        start_caches(2)
     if layer == 0:
         for copy in x_copies:
             copy.wait()
     for c in range(CHUNKS):
         first_finish(c)
+        start_caches(2)
     for copy in copies:
         copy.wait()
     for c in range(CHUNKS):
@@ -399,9 +418,12 @@
         arrived(0, c)
         mlp(c)
         send_pairs(1, c)
+        start_caches(2)
     add_pairs(1, CHUNKS - 1)
+    start_caches(2)
     for c in range(CHUNKS):
         second_finish(c)
+        start_caches(2 if c == 0 else 2 * PIECES)
     for c in range(CHUNKS):
         forward(1, c)
     for c in range(CHUNKS):
@@ -493,7 +515,7 @@
             rows, *held = mlp_block(layer, last, part, own, norm_gain, norm_bias, b_out, b_up, b_down, w_up, w_down, k_in, v_in)
             if not last:
                 own, k_next, v_next = held
-                caches = (pltpu.with_memory_space_constraint(k_next, pltpu.VMEM), pltpu.with_memory_space_constraint(v_next, pltpu.VMEM), k_out, v_out)
+                caches = (in_vmem(k_next), in_vmem(v_next), k_out, v_out)
 
         def back(cache):
             return jnp.swapaxes(cache.reshape(layers, batch, heads, head, slots), 3, 4)

time: 130 us -> 125 us (0.962)
  Pallas kernels: 126 us -> 122 us
    pallas_call x2, Pallas kernels: 77.7 us -> 72.6 us  [mlp_block(): pl.pallas_call(functools.partial(mlp_kernel, layer, last), out_shape=out_...]
where the time goes in v3:
time: 125 us
  Pallas kernels  122 us (98%)
  local copies, waits for them, and re-layouts  2.3 us (2%)
    pallas_call x2, Pallas kernels, mlp_block(): pl.pallas_call(functools.partial(mlp_kernel, layer, last), out_shape=out_...  72.6 us
    pallas_call x2, Pallas kernels, attention(): pl.pallas_call(functools.partial(attention_kernel, layer, fetch), out_sha...  49.4 us

profile of v3, /device:TPU:0, one launch (start us, length us, event | category | flops | bytes accessed | tf_op | source)
XLA Modules:
  0.0 124.9 jit_solution(13957113031634779793)
XLA Ops:
  0.6 26.0 %attention_0.1 = (bf16[2,256,256,128]{3,2,1,0:T(8,128)(2,1)}, bf16[2,256,256,128]{3,2,1,0:T(8,128)(2,1)}, bf16[256,2048]{1,0:T(8,128)(2,1)}) custom-call(s32[256]{0:T(256)} %lens.3, bf16[256,2048]{1,0:T(8,128)(2,1)} %x_ref.1, f32[2,2,2048]{2,1,0:T(2,128)} %gain_ref.7, f32[2,2,2048]{2,1,0:T(2,128)} %bias_ref.7, bf16[2,3,4,64]{3,2,1,0:T(4,128)(2,1)} %bqkv_ref.3, ...), custom_call_target="tpu_custom_call" | custom-call | tf_op jit(solution)/shard_map/attention_0/pallas_call | solution.py:218
  26.7 37.2 %mlp_0.1 = (bf16[256,2048]{1,0:T(8,128)(2,1)}, bf16[2,16,2048]{2,1,0:T(8,128)(2,1)}, bf16[256,256,128]{2,1,0:T(8,128)(2,1)S(1)}, bf16[256,256,128]{2,1,0:T(8,128)(2,1)S(1)}) custom-call(bf16[256,2048]{1,0:T(8,128)(2,1)} %get-tuple-element.13.part_ref, bf16[256,2048]{1,0:T(8,128)(2,1)} %x_ref.1, f32[2,2,2048]{2,1,0:T(2,128)} %gain_ref.7, ...), custom_call_target="tpu_custom_call" | custom-call | tf_op jit(solution)/shard_map/mlp_0/pallas_call | solution.py:460
  63.9 23.3 %attention_1.1 = (bf16[2,256,256,128]{3,2,1,0:T(8,128)(2,1)}, bf16[2,256,256,128]{3,2,1,0:T(8,128)(2,1)}, bf16[256,2048]{1,0:T(8,128)(2,1)}) custom-call(s32[256]{0:T(256)} %lens.3, bf16[256,2048]{1,0:T(8,128)(2,1)} %get-tuple-element.14.x_hbm, f32[2,2,2048]{2,1,0:T(2,128)} %gain_ref.7, ...), custom_call_target="tpu_custom_call", output_to_operand_aliasing={{0}: (9, {}), {1}: (10, {})} | custom-call | tf_op jit(solution)/shard_map/attention_1/pallas_call | solution.py:218
  87.2 35.4 %mlp_1.1 = bf16[256,2048]{1,0:T(8,128)(2,1)} custom-call(bf16[256,2048]{1,0:T(8,128)(2,1)} %get-tuple-element.19.part_ref, bf16[2,16,2048]{2,1,0:T(8,128)(2,1)} %get-tuple-element.20.x_ref, f32[2,2,2048]{2,1,0:T(2,128)} %gain_ref.7, f32[2,2,2048]{2,1,0:T(2,128)} %bias_ref.7, bf16[2,2048]{1,0:T(2,128)(2,1)} %bout_ref.3, bf16[2,1024]{1,0:T(2,128)(2,1)} %bup_ref.3, ...), custom_call_target="tpu_custom_call" | custom-call | tf_op jit(solution)/shard_map/mlp_1/pallas_call | solution.py:460
  122.6 2.3 %copy.22 = bf16[256,2048]{1,0:T(8,128)(2,1)} copy(bf16[256,2048]{1,0:T(8,128)(2,1)} %mlp_1.1) | data formatting | bytes 2097152

commit v4 on v3

--- a/solution.py
+++ b/solution.py
@@ -17,6 +17,7 @@
 GROUP = 16
 RING = 3
 PIECES = 8
+UPDATES = (4, 1, 1, 2, 3, 3, 2)
 CHUNKS = 2
 
 
@@ -249,22 +250,22 @@
     )(*args)
 
 
-def in_vmem(array):
-    return pltpu.with_memory_space_constraint(array, pltpu.VMEM)
-
-
-def mlp_kernel(layer, last, part_ref, x_ref, gain_ref, bias_ref, bout_ref, bup_ref, bdown_ref, wup_hbm, wdown_hbm, *rest):
-    if last:
-        full_ref, rest = rest[0], rest[1:]
-    else:
-        k_hbm, v_hbm, full_ref, own_ref, k_next, v_next = rest[:6]
-        rest = rest[6:]
-    (wup, wdown, part2, hbuf, ubuf, pair_in, cross_out, cross_in, own_sum, xown,
-     w_sem, pair_s, pair_r, cross_s, cross_r, gat_s, gat_r, fwd_s, fwd_r, cache_sem) = rest
+def middle_kernel(lens, part_ref, x_hbm, gain_ref, bias_ref, bqkv_ref, bout_ref, bup_ref, bdown_ref,
+                  wqkv_hbm, wout_hbm, wup_hbm, wdown_hbm, k_hbm, v_hbm,
+                  full_ref, keys, values,
+                  wqkv, wout, wup, wdown, parts, hbuf, ubuf, pair_in, cross_out, cross_in, own_sum, xown,
+                  qrep, kcols, vcols, vrows, sbuf, abuf,
+                  w_sem, cache_sem, pair_s, pair_r, cross_s, cross_r, gat_s, gat_r, fwd_s, fwd_r):
     batch, width = part_ref.shape
     hidden = wup.shape[1]
+    hd = wout.shape[0]
+    head = hd // 4
+    slots = keys.shape[2]
     rows_c = batch // CHUNKS
     rows_o = rows_c // 8
+    n = GROUP * 4
+    groups_c = rows_c // GROUP
+    scale = head ** -0.5
     me = lax.axis_index("tp")
     core = lax.rem(me, 2)
     chip = lax.div(me, 2)
@@ -273,28 +274,22 @@
     partner = chip * 2 + 1 - core
     chips = ((1 - cy) * 2 + 1 - cx, cy * 2 + 1 - cx, (1 - cy) * 2 + cx, chip)
 
-    def device(index):
-        return {"tp": index}
-
     def rows_of(c, owner):
         return pl.ds(pl.multiple_of(c * rows_c + owner * rows_o, rows_o), rows_o)
 
-    barrier = pltpu.get_barrier_semaphore()
-    for peer in (partner,) + tuple(t * 2 + core for t in chips[:3]):
-        pl.semaphore_signal(barrier, inc=1, device_id=device(peer), device_id_type=MESH)
-    pl.semaphore_wait(barrier, 4)
-
     def remote(src, dst, send, recv, target):
         return pltpu.make_async_remote_copy(
-            src_ref=src, dst_ref=dst, send_sem=send, recv_sem=recv, device_id=device(target), device_id_type=MESH)
+            src_ref=src, dst_ref=dst, send_sem=send, recv_sem=recv, device_id={"tp": target}, device_id_type=MESH)
+
+    def source(s):
+        return part_ref if s == 0 else parts.at[s - 1]
 
     def pair_copy(s, c, k):
-        src = part_ref if s == 0 else part2
-        return remote(src.at[rows_of(c, chips[k] * 2 + 1 - core)], pair_in.at[s, c, k],
+        return remote(source(s).at[rows_of(c, chips[k] * 2 + 1 - core)], pair_in.at[s % 2, c, k],
                       pair_s.at[s, c, k], pair_r.at[s, c, k], partner)
 
     def cross_copy(s, c, k):
-        return remote(cross_out.at[s, c, k], cross_in.at[s, c, k],
+        return remote(cross_out.at[s % 2, c, k], cross_in.at[s % 2, c, k],
                       cross_s.at[s, c, k], cross_r.at[s, c, k], chips[k] * 2 + core)
 
     def gather_copy(s, c, k):
@@ -311,24 +306,33 @@
             pair_copy(s, c, k).start()
 
     def add_pairs(s, c):
-        src = part_ref if s == 0 else part2
         for k in range(4):
             pair_copy(s, c, k).wait_recv()
-            both = src[rows_of(c, chips[k] * 2 + core), :].astype(F32) + pair_in[s, c, k].astype(F32)
+            both = source(s)[rows_of(c, chips[k] * 2 + core), :].astype(F32) + pair_in[s % 2, c, k].astype(F32)
             if k < 3:
-                cross_out[s, c, k] = both.astype(BF16)
+                if s > 1:
+                    cross_copy(s - 2, c, k).wait_send()
+                cross_out[s % 2, c, k] = both.astype(BF16)
                 cross_copy(s, c, k).start()
             else:
                 own_sum[c] = both
 
-    def own_total(s, c):
+    def row(ref, index):
+        return ref[index:index + 1, :].astype(F32)
+
+    def finish(s, c):
+        layer = s // 2
         total = own_sum[c]
         for k in (1, 2, 0):
             cross_copy(s, c, k).wait_recv()
-            total = total + cross_in[s, c, k].astype(F32)
-        return total
-
-    def send_own(s, c):
+            total = total + cross_in[s % 2, c, k].astype(F32)
+        add = row(bout_ref, layer) if s % 2 == 0 else row(bdown_ref, layer)
+        new = (xown[c].astype(F32) + total + add).astype(BF16)
+        if s < 3:
+            xown[c] = new
+            at = s + 1
+            new = norm(new.astype(F32), gain_ref[at // 2, at % 2:at % 2 + 1, :], bias_ref[at // 2, at % 2:at % 2 + 1, :]).astype(BF16)
+        hbuf[s, rows_of(c, me), :] = new
         for k in range(4):
             gather_copy(s, c, k).start()
 
@@ -342,152 +346,320 @@
         for k in range(3):
             forward_copy(s, c, k).wait_recv()
 
-    def row(ref, index):
-        return ref[index:index + 1, :].astype(F32)
-
-    def first_finish(c):
-        total = own_total(0, c)
-        old = xown[c] if layer == 0 else x_ref[c]
-        mid = (old.astype(F32) + total + row(bout_ref, layer)).astype(BF16)
-        xown[c] = mid
-        hbuf[0, rows_of(c, me), :] = norm(mid.astype(F32), gain_ref[layer, 1:2, :], bias_ref[layer, 1:2, :]).astype(BF16)
-        send_own(0, c)
-
-    def second_finish(c):
-        total = own_total(1, c)
-        new = (xown[c].astype(F32) + total + row(bdown_ref, layer)).astype(BF16)
-        if last:
-            hbuf[1, rows_of(c, me), :] = new
-        else:
-            own_ref[c] = new
-            hbuf[1, rows_of(c, me), :] = norm(new.astype(F32), gain_ref[layer + 1, 0:1, :], bias_ref[layer + 1, 0:1, :]).astype(BF16)
-        send_own(1, c)
-
-    def mlp(c):
+    def mlp(layer, c):
+        s = 2 * layer
         rows = slice(c * rows_c, (c + 1) * rows_c)
-        h = hbuf[0, rows, :]
-        for n in range(0, hidden, 256):
-            up = dot(h, wup[:, n:n + 256]) + bup_ref[layer:layer + 1, n:n + 256].astype(F32)
-            ubuf[:, n:n + 256] = jnp.maximum(up, 0.0).astype(BF16)
+        h = hbuf[s, rows, :]
+        for i in range(0, hidden, 256):
+            up = dot(h, wup[:, i:i + 256]) + bup_ref[layer:layer + 1, i:i + 256].astype(F32)
+            ubuf[:, i:i + 256] = jnp.maximum(up, 0.0).astype(BF16)
         u = ubuf[...]
-        for n in range(0, width, 256):
-            part2[rows, n:n + 256] = dot(u, wdown[:, n:n + 256]).astype(BF16)
-
+        for i in range(0, width, 256):
+            parts[s, rows, i:i + 256] = dot(u, wdown[:, i:i + 256]).astype(BF16)
+
+    spread_cols = (lax.broadcasted_iota(jnp.int32, (head, hd), 0) == lax.broadcasted_iota(jnp.int32, (head, hd), 1) % head).astype(F32).astype(BF16)
+    head_of = lax.broadcasted_iota(jnp.int32, (4, hd), 0) == lax.broadcasted_iota(jnp.int32, (4, hd), 1) // head
+    own_head = lax.broadcasted_iota(jnp.int32, (n, hd), 0) % 4 == lax.broadcasted_iota(jnp.int32, (n, hd), 1) // head
+    repeat = (lax.broadcasted_iota(jnp.int32, (n, GROUP), 0) // 4 == lax.broadcasted_iota(jnp.int32, (n, GROUP), 1)).astype(F32).astype(BF16)
+    collect = (lax.broadcasted_iota(jnp.int32, (GROUP, n), 1) // 4 == lax.broadcasted_iota(jnp.int32, (GROUP, n), 0)).astype(F32).astype(BF16)
+    top8 = lax.broadcasted_iota(jnp.int32, (8, slots), 0) < 4
+    lane = lax.broadcasted_iota(jnp.int32, (n, slots), 1)
+    row_seq = lax.broadcasted_iota(jnp.int32, (n, slots), 0) // 4
+    lane16 = lax.broadcasted_iota(jnp.int32, (16, slots), 1).astype(F32).astype(BF16)
+
+    def bias_row(part):
+        wide = dot(bqkv_ref[1, part], spread_cols)
+        return jnp.sum(jnp.where(head_of, wide, 0.0), axis=0, keepdims=True)
+
+    def project(c):
+        rows = slice(c * rows_c, (c + 1) * rows_c)
+        h = hbuf[1, rows, :]
+        q = (dot(h, wqkv[0:hd, :], NT) + bias_row(0)).astype(BF16)
+        for g in range(groups_c):
+            at = (c * groups_c + g) * n
+            qrep[at:at + n, :] = jnp.where(own_head, dot(repeat, q[g * GROUP:(g + 1) * GROUP, :]), 0.0).astype(BF16)
+        for part, cols in ((1, kcols), (2, vcols)):
+            column = jnp.broadcast_to(bias_row(part), (128, hd)).T
+            new = (dot(wqkv[part * hd:(part + 1) * hd, :], h, NT) + column).astype(BF16)
+            cols[c] = new
+            if part == 2:
+                vrows[rows, :] = new.astype(F32).T.astype(BF16)
+
+    def lengths(g):
+        base = g * GROUP
+        return jnp.concatenate([jnp.where(top8, lens[base + i], lens[base + i + 1]) for i in range(0, GROUP, 2)], axis=0)
+
+    def stage(c, key_group, value_group):
+        if value_group is not None:
+            scores = sbuf[lax.rem(value_group, 2)]
+            weights = jnp.exp(scores - jnp.max(scores, axis=-1, keepdims=True))
+            prob = (weights / jnp.sum(weights, axis=-1, keepdims=True)).astype(BF16).astype(F32)
+            at_new = lane == lengths(value_group)
+            prob_new = jnp.sum(jnp.where(at_new, prob, 0.0), axis=-1, keepdims=True)
+            prob = jnp.where(at_new, 0.0, prob)
+        if key_group is not None:
+            q_rows = qrep[pl.ds(pl.multiple_of(key_group * n, n), n), :]
+        raw, outs = [], []
+        for i in range(0, GROUP, 2):
+            if key_group is not None:
+                tiles = [keys[key_group * GROUP + b] for b in (i, i + 1)]
+                both = dot(q_rows[i * 4:i * 4 + 8, :], jnp.concatenate(tiles, axis=1))
+                raw.append(jnp.where(top8, both[:, 0:slots], both[:, slots:2 * slots]))
+            if value_group is not None:
+                tiles = [values[value_group * GROUP + b] for b in (i, i + 1)]
+                pair = prob[i * 4:i * 4 + 8, :]
+                spread = jnp.concatenate([jnp.where(top8, pair, 0.0), jnp.where(top8, 0.0, pair)], axis=1).astype(BF16)
+                outs.append(dot(spread, jnp.concatenate(tiles, axis=1), NT))
+        if key_group is not None:
+            cross = dot(q_rows, kcols[c])
+            mine = lane == row_seq + (key_group - c * groups_c) * GROUP
+            score_new = jnp.sum(jnp.where(mine, cross, 0.0), axis=-1, keepdims=True)
+            limit = lengths(key_group)
+            score = jnp.where(lane == limit, score_new, jnp.concatenate(raw, axis=0)) * scale
+            sbuf[lax.rem(key_group, 2)] = jnp.where(lane <= limit, score, -1e30)
+        if value_group is not None:
+            v_rep = dot(repeat, vrows[pl.ds(pl.multiple_of(value_group * GROUP, GROUP), GROUP), :])
+            heads = jnp.where(own_head, jnp.concatenate(outs, axis=0) + prob_new * v_rep, 0.0).astype(BF16)
+            abuf[pl.ds(pl.multiple_of(value_group * GROUP, GROUP), GROUP), :] = dot(collect, heads).astype(BF16)
+
+    def attend(c):
+        first, end = c * groups_c, (c + 1) * groups_c
+        stage(c, jnp.int32(first), None)
+
+        def step(g, carry):
+            stage(c, g, g - 1)
+            return carry
+
+        lax.fori_loop(first + 1, end, step, 0)
+        stage(c, None, jnp.int32(end - 1))
+        rows = slice(c * rows_c, (c + 1) * rows_c)
+        a = abuf[rows, :]
+        for i in range(0, width, 512):
+            parts[1, rows, i:i + 512] = dot(a, wout[:, i:i + 512]).astype(BF16)
+
+    def update(count):
+        lo = done[0]
+        done[0] += count
+
+        def group(g, carry):
+            base = g * GROUP
+            page = lax.div(g, groups_c)
+            turn = 128 - lax.rem(g, groups_c) * GROUP
+            k_cols = pltpu.roll(kcols[page].astype(F32), turn, 1)
+            v_cols = pltpu.roll(vcols[page].astype(F32), turn, 1)
+            for b in range(GROUP):
+                here = lane16 == jnp.full((16, slots), lens[base + b].astype(F32), F32).astype(BF16)
+                for cols, ref in ((k_cols, keys), (v_cols, values)):
+                    column = jnp.broadcast_to(cols[:, b:b + 1], (hd, slots)).astype(BF16).reshape(hd // 16, 16, slots)
+                    old = ref[base + b].reshape(hd // 16, 16, slots)
+                    ref[base + b] = jnp.where(here[None], column, old).reshape(hd, slots)
+            return carry
+
+        lax.fori_loop(lo, lo + count, group, 0)
+
+    done = [0]
+
+    x_copies = [pltpu.make_async_copy(x_hbm.at[rows_of(c, me)], xown.at[c], w_sem.at[c]) for c in range(CHUNKS)]
+    up_copies = [[pltpu.make_async_copy(wup_hbm.at[l], wup, w_sem.at[2 + 2 * l]),
+                  pltpu.make_async_copy(wdown_hbm.at[l], wdown, w_sem.at[3 + 2 * l])] for l in range(2)]
+    qkv_copies = [pltpu.make_async_copy(wqkv_hbm.at[1], wqkv, w_sem.at[6]), pltpu.make_async_copy(wout_hbm.at[1], wout, w_sem.at[7])]
+    piece = batch // PIECES
+    caches = []
+    for p in range(PIECES):
+        rows = slice(p * piece, (p + 1) * piece)
+        caches.append(pltpu.make_async_copy(k_hbm.at[1, rows], keys.at[rows], cache_sem.at[0, p]))
+        caches.append(pltpu.make_async_copy(v_hbm.at[1, rows], values.at[rows], cache_sem.at[1, p]))
+    pending = list(caches)
+
+    def start_caches(count):
+        for copy in pending[:count]:
+            copy.start()
+        del pending[:count]
+
+    results = []
     for c in range(CHUNKS):
-        send_pairs(0, c)
-    copies = [
-        pltpu.make_async_copy(wup_hbm.at[layer], wup, w_sem.at[0]),
-        pltpu.make_async_copy(wdown_hbm.at[layer], wdown, w_sem.at[1]),
-    ]
-    for copy in copies:
-        copy.start()
-    if layer == 0:
-        x_copies = [pltpu.make_async_copy(x_ref.at[rows_of(c, me)], xown.at[c], w_sem.at[2 + c]) for c in range(CHUNKS)]
-        for copy in x_copies:
-            copy.start()
-
-    caches = []
-    if not last:
-        piece = batch // PIECES
-        for p in range(PIECES):
-            rows = slice(p * piece, (p + 1) * piece)
-            caches.append(pltpu.make_async_copy(k_hbm.at[layer + 1, rows], k_next.at[rows], cache_sem.at[0, p]))
-            caches.append(pltpu.make_async_copy(v_hbm.at[layer + 1, rows], v_next.at[rows], cache_sem.at[1, p]))
-    started = []
-
-    def start_caches(count):
-        for copy in caches[len(started):len(started) + count]:
-            copy.start()
-            started.append(copy)
-
+        rows = slice(c * rows_c, (c + 1) * rows_c)
+        results.append(pltpu.make_async_copy(hbuf.at[3, rows], full_ref.at[rows], w_sem.at[8 + c]))
+
+    def run(copies, wait):
+        for copy in copies:
+            if wait:
+                copy.wait()
+            else:
+                copy.start()
+
+    barrier = pltpu.get_barrier_semaphore()
+    for peer in (partner,) + tuple(t * 2 + core for t in chips[:3]):
+        pl.semaphore_signal(barrier, inc=1, device_id={"tp": peer}, device_id_type=MESH)
+    pl.semaphore_wait(barrier, 4)
+
+    send_pairs(0, 0)
+    send_pairs(0, 1)
+    run(x_copies, False)
+    run(up_copies[0], False)
+    run(qkv_copies, False)
+    add_pairs(0, 0)
+    add_pairs(0, 1)
+    start_caches(2)
+    run(x_copies, True)
+    finish(0, 0)
+    start_caches(2)
+    finish(0, 1)
+    start_caches(2)
+    run(up_copies[0], True)
+    forward(0, 0)
+    start_caches(1)
+    arrived(0, 0)
+    mlp(0, 0)
+    send_pairs(1, 0)
+    forward(0, 1)
+    add_pairs(1, 0)
+    start_caches(1)
+    arrived(0, 1)
+    mlp(0, 1)
+    send_pairs(1, 1)
+    start_caches(2)
+    add_pairs(1, 1)
+    run(up_copies[1], False)
+    start_caches(2)
+    finish(1, 0)
+    start_caches(2)
+    finish(1, 1)
+    start_caches(2)
+    run(qkv_copies, True)
+    forward(1, 0)
+    arrived(1, 0)
+    project(0)
+    forward(1, 1)
+    run(caches, True)
+    attend(0)
+    send_pairs(2, 0)
+    arrived(1, 1)
+    project(1)
+    add_pairs(2, 0)
+    attend(1)
+    send_pairs(2, 1)
+    finish(2, 0)
+    add_pairs(2, 1)
+    update(UPDATES[0])
+    finish(2, 1)
+    run(up_copies[1], True)
+    update(UPDATES[1])
+    forward(2, 0)
+    arrived(2, 0)
+    mlp(1, 0)
+    send_pairs(3, 0)
+    forward(2, 1)
+    add_pairs(3, 0)
+    arrived(2, 1)
+    mlp(1, 1)
+    send_pairs(3, 1)
+    update(UPDATES[2])
+    add_pairs(3, 1)
+    update(UPDATES[3])
+    finish(3, 0)
+    update(UPDATES[4])
+    finish(3, 1)
+    update(UPDATES[5])
+    forward(3, 0)
+    update(UPDATES[6])
+    forward(3, 1)
     for c in range(CHUNKS):
-        add_pairs(0, c)
-        start_caches(2)
-    if layer == 0:
-        for copy in x_copies:
-            copy.wait()
-    for c in range(CHUNKS):
-        first_finish(c)
-        start_caches(2)
-    for copy in copies:
-        copy.wait()
-    for c in range(CHUNKS):
-        forward(0, c)
-        if c > 0:
-            add_pairs(1, c - 1)
-        arrived(0, c)
-        mlp(c)
-        send_pairs(1, c)
-        start_caches(2)
-    add_pairs(1, CHUNKS - 1)
-    start_caches(2)
-    for c in range(CHUNKS):
-        second_finish(c)
-        start_caches(2 if c == 0 else 2 * PIECES)
-    for c in range(CHUNKS):
-        forward(1, c)
-    for c in range(CHUNKS):
-        arrived(1, c)
-        rows = slice(c * rows_c, (c + 1) * rows_c)
-        full_ref[rows, :] = hbuf[1, rows, :]
-    for copy in caches:
-        copy.wait()
-    for s in range(2):
+        arrived(3, c)
+        results[c].start()
+    run(results, True)
+    for s in range(4):
         for c in range(CHUNKS):
             for k in range(4):
                 pair_copy(s, c, k).wait_send()
                 gather_copy(s, c, k).wait_send()
                 if k < 3:
-                    cross_copy(s, c, k).wait_send()
+                    if s > 1:
+                        cross_copy(s, c, k).wait_send()
                     forward_copy(s, c, k).wait_send()
 
 
-def mlp_block(layer, last, part, x, gains, biases, bout, bup, bdown, wup, wdown, k_in, v_in):
+def middle(lens, part, x, gains, biases, bqkv, bout, bup, bdown, wqkv, wout, wup, wdown, k_in, v_in):
     batch, width = part.shape
     hidden = wup.shape[2]
+    hd, slots = k_in.shape[2:]
     rows_o = batch // CHUNKS // 8
     any_spec = pl.BlockSpec(memory_space=pl.ANY)
     vmem_spec = pl.BlockSpec(memory_space=pltpu.VMEM)
     own = (CHUNKS, rows_o, width)
-    args = [part, x, gains, biases, bout, bup, bdown, wup, wdown]
-    in_specs = [vmem_spec, any_spec if layer == 0 else vmem_spec] + [vmem_spec] * 5 + [any_spec] * 2
-    out_shape = [jax.ShapeDtypeStruct((batch, width), BF16)]
-    if not last:
-        args += [k_in, v_in]
-        in_specs += [any_spec] * 2
-        out_shape += [jax.ShapeDtypeStruct(own, BF16), pltpu.VMEM(k_in.shape[1:], BF16), pltpu.VMEM(v_in.shape[1:], BF16)]
     dma = pltpu.SemaphoreType.DMA
     return pl.pallas_call(
-        functools.partial(mlp_kernel, layer, last),
-        out_shape=out_shape,
-        in_specs=in_specs,
-        out_specs=[vmem_spec] * len(out_shape),
+        middle_kernel,
+        out_shape=(jax.ShapeDtypeStruct((batch, width), BF16), pltpu.VMEM(k_in.shape[1:], BF16), pltpu.VMEM(v_in.shape[1:], BF16)),
+        in_specs=[pl.BlockSpec(memory_space=pltpu.SMEM), vmem_spec, any_spec] + [vmem_spec] * 6 + [any_spec] * 6,
+        out_specs=(any_spec, vmem_spec, vmem_spec),
         scratch_shapes=[
+            pltpu.VMEM((3 * hd, width), BF16),
+            pltpu.VMEM((hd, width), BF16),
             pltpu.VMEM((width, hidden), BF16),
             pltpu.VMEM((hidden, width), BF16),
-            pltpu.VMEM((batch, width), BF16),
-            pltpu.VMEM((2, batch, width), BF16),
+            pltpu.VMEM((3, batch, width), BF16),
+            pltpu.VMEM((4, batch, width), BF16),
             pltpu.VMEM((batch // CHUNKS, hidden), BF16),
             pltpu.VMEM((2, CHUNKS, 4, rows_o, width), BF16),
             pltpu.VMEM((2, CHUNKS, 3, rows_o, width), BF16),
             pltpu.VMEM((2, CHUNKS, 3, rows_o, width), BF16),
             pltpu.VMEM(own, F32),
             pltpu.VMEM(own, BF16),
-            dma((2 + CHUNKS,)),
-            dma((2, CHUNKS, 4)),
-            dma((2, CHUNKS, 4)),
-            dma((2, CHUNKS, 3)),
-            dma((2, CHUNKS, 3)),
-            dma((2, CHUNKS, 4)),
-            dma((2, CHUNKS, 4)),
-            dma((2, CHUNKS, 3)),
-            dma((2, CHUNKS, 3)),
+            pltpu.VMEM((batch * 4, hd), BF16),
+            pltpu.VMEM((CHUNKS, hd, 128), BF16),
+            pltpu.VMEM((CHUNKS, hd, 128), BF16),
+            pltpu.VMEM((batch, hd), BF16),
+            pltpu.VMEM((2, GROUP * 4, slots), F32),
+            pltpu.VMEM((batch, hd), BF16),
+            dma((8 + CHUNKS,)),
             dma((2, PIECES)),
+            dma((4, CHUNKS, 4)),
+            dma((4, CHUNKS, 4)),
+            dma((4, CHUNKS, 3)),
+            dma((4, CHUNKS, 3)),
+            dma((4, CHUNKS, 4)),
+            dma((4, CHUNKS, 4)),
+            dma((4, CHUNKS, 3)),
+            dma((4, CHUNKS, 3)),
         ],
         compiler_params=pltpu.CompilerParams(
-            collective_id=layer, has_side_effects=True, vmem_limit_bytes=(60 if last else 24) * 1024 * 1024),
-        name=f"mlp_{layer}",
-    )(*args)
+            collective_id=0, has_side_effects=True, vmem_limit_bytes=25 * 1024 * 1024),
+        name="middle",
+    )(lens, part, x, gains, biases, bqkv, bout, bup, bdown, wqkv, wout, wup, wdown, k_in, v_in)
+
+
+def write_kernel(x_ref, keys, values, k_old, v_old, x_out, k_out, v_out, sem):
+    piece = keys.shape[0] // PIECES
+    copies = []
+    for p in range(PIECES):
+        rows = slice(p * piece, (p + 1) * piece)
+        copies.append(pltpu.make_async_copy(keys.at[rows], k_out.at[1, rows], sem.at[0, p]))
+        copies.append(pltpu.make_async_copy(values.at[rows], v_out.at[1, rows], sem.at[1, p]))
+    for copy in copies:
+        copy.start()
+    x_out[...] = x_ref[...]
+    for copy in copies:
+        copy.wait()
+
+
+def write(x, keys, values, k_out, v_out):
+    any_spec = pl.BlockSpec(memory_space=pl.ANY)
+    vmem_spec = pl.BlockSpec(memory_space=pltpu.VMEM)
+    return pl.pallas_call(
+        write_kernel,
+        out_shape=(jax.ShapeDtypeStruct(x.shape, BF16), jax.ShapeDtypeStruct(k_out.shape, BF16), jax.ShapeDtypeStruct(v_out.shape, BF16)),
+        in_specs=[vmem_spec] * 3 + [any_spec] * 2,
+        out_specs=(vmem_spec, any_spec, any_spec),
+        input_output_aliases={3: 1, 4: 2},
+        scratch_shapes=[pltpu.SemaphoreType.DMA((2, PIECES))],
+        compiler_params=pltpu.CompilerParams(vmem_limit_bytes=25 * 1024 * 1024),
+        name="write",
+    )(x, in_vmem(keys), in_vmem(values), k_out, v_out)
+
+
+def in_vmem(array):
+    return pltpu.with_memory_space_constraint(array, pltpu.VMEM)
 
 
 def solution(mesh):
@@ -507,15 +679,9 @@
         wqkv = jnp.transpose(w_qkv, (0, 2, 3, 4, 1)).reshape(layers, 3 * hd, width)
         wout = w_out.reshape(layers, hd, width)
 
-        rows, own = x, x
-        caches = (k_in, v_in)
-        for layer in range(layers):
-            k_out, v_out, part = attention(layer, layer == 0, cache_len, rows, norm_gain, norm_bias, b_qkv, wqkv, wout, *caches)
-            last = layer == layers - 1
-            rows, *held = mlp_block(layer, last, part, own, norm_gain, norm_bias, b_out, b_up, b_down, w_up, w_down, k_in, v_in)
-            if not last:
-                own, k_next, v_next = held
-                caches = (in_vmem(k_next), in_vmem(v_next), k_out, v_out)
+        k_out, v_out, part = attention(0, True, cache_len, x, norm_gain, norm_bias, b_qkv, wqkv, wout, k_in, v_in)
+        rows, keys, values = middle(cache_len, part, x, norm_gain, norm_bias, b_qkv, b_out, b_up, b_down, wqkv, wout, w_up, w_down, k_in, v_in)
+        rows, k_out, v_out = write(rows, keys, values, k_out, v_out)
 
         def back(cache):
             return jnp.swapaxes(cache.reshape(layers, batch, heads, head, slots), 3, 4)

time: 125 us -> 121 us (0.968)
  local copies, waits for them, and re-layouts: 2.3 us -> 0 us
  Pallas kernels: 122 us -> 120 us
    pallas_call x2 -> x1, Pallas kernels: 49.4 us -> 26 us  [attention(): pl.pallas_call(functools.partial(attention_kernel, layer, fetch), out_sha...]
    pallas_call x2, Pallas kernels: 72.6 us -> 94.1 us  [the longest x1 80.8 us: middle(): pl.pallas_call(middle_kernel, out_shape=(jax.ShapeDtypeStruct((batch, wid...]
    unnamed x1 -> x0, local copies, waits for them, and re-layouts: 2.3 us -> none
where the time goes in v4:
time: 121 us
  Pallas kernels  120 us (99%)
    pallas_call x1, Pallas kernels, middle(): pl.pallas_call(middle_kernel, out_shape=(jax.ShapeDtypeStruct((batch, wid...  80.8 us
    pallas_call x1, Pallas kernels, attention(): pl.pallas_call(functools.partial(attention_kernel, layer, fetch), out_sha...  26 us
    pallas_call x1, Pallas kernels, write(): pl.pallas_call(write_kernel, out_shape=(jax.ShapeDtypeStruct(x.shape, BF1...  13.2 us

profile of v4, /device:TPU:0, one launch (start us, length us, event | category | flops | bytes accessed | tf_op | source)
XLA Modules:
  0.0 120.9 jit_solution(4735829138971662415)
XLA Ops:
  0.6 26.0 %attention_0.1 = (bf16[2,256,256,128]{3,2,1,0:T(8,128)(2,1)}, bf16[2,256,256,128]{3,2,1,0:T(8,128)(2,1)}, bf16[256,2048]{1,0:T(8,128)(2,1)}) custom-call(s32[256]{0:T(256)} %lens.3, bf16[256,2048]{1,0:T(8,128)(2,1)} %x_hbm.3, f32[2,2,2048]{2,1,0:T(2,128)} %gain_ref.3, f32[2,2,2048]{2,1,0:T(2,128)} %bias_ref.3, bf16[2,3,4,64]{3,2,1,0:T(4,128)(2,1)} %bqkv_ref.3, ...), custom_call_target="tpu_custom_call" | custom-call | tf_op jit(solution)/shard_map/attention_0/pallas_call | solution.py:219
  26.7 80.8 %middle.1 = (bf16[256,2048]{1,0:T(8,128)(2,1)}, bf16[256,256,128]{2,1,0:T(8,128)(2,1)S(1)}, bf16[256,256,128]{2,1,0:T(8,128)(2,1)S(1)}) custom-call(s32[256]{0:T(256)} %lens.3, bf16[256,2048]{1,0:T(8,128)(2,1)} %get-tuple-element.12.part_ref, bf16[256,2048]{1,0:T(8,128)(2,1)} %x_hbm.3, f32[2,2,2048]{2,1,0:T(2,128)} %gain_ref.3, f32[2,2,2048]{2,1,0:T(2,128)} %bias_ref.3, ...), custom_call_target="tpu_custom_call" | custom-call | tf_op jit(solution)/shard_map/middle/pallas_call | solution.py:591
  107.5 13.2 %write.1 = (bf16[256,2048]{1,0:T(8,128)(2,1)}, bf16[2,256,256,128]{3,2,1,0:T(8,128)(2,1)}, bf16[2,256,256,128]{3,2,1,0:T(8,128)(2,1)}) custom-call(bf16[256,2048]{1,0:T(8,128)(2,1)} %get-tuple-element.13.x_ref, bf16[256,256,128]{2,1,0:T(8,128)(2,1)S(1)} %get-tuple-element.14.keys, ...), custom_call_target="tpu_custom_call", output_to_operand_aliasing={{1}: (3, {}), {2}: (4, {})} | custom-call | tf_op jit(solution)/shard_map/write/pallas_call | solution.py:649
